TPU v7x, 256 devices: a 4x2x16 block of a 4x16x16 slice. The times are simulated.
256 devices in a mesh: groups: 2 (over y), tp: 16 (over z), tq: 4 (over x), tr: 2 (over core).
Axes of the slice: x: 4, y: 2, z: 16, core: 2. Of those that a mesh axis runs over, the one named last changes fastest.
The devices are a block of a 4x16x16 slice.
Arguments:
- attn_heads: bfloat16 [128, 16384], P('groups', ('tp', 'tq', 'tr')), parts along dimension 0, may hold values from -6 to 6
- residual: bfloat16 [128, 16384], P('groups', ('tp', 'tq', 'tr')), parts along dimension 0, may hold values from -120 to 120
- o_weight: bfloat16 [16384, 16384], P(('tp', 'tq', 'tr')), may hold values from -0.1875 to 0.1875
- norm_gain: bfloat16 [16384], P(('tp', 'tq', 'tr')), may hold values from 0.099609375 to 1.8984375
- q_weight: bfloat16 [16384, 16384], P(None, ('tp', 'tq', 'tr')), may hold values from -0.046875 to 0.046875
Outputs:
- hidden: bfloat16 [128, 16384], P('groups', ('tp', 'tq', 'tr')), parts along dimension 0
- peak_value: float32 [128], P('groups'), parts along dimension 0
- query: bfloat16 [128, 16384], P('groups', ('tp', 'tq', 'tr')), parts along dimension 0
There are 2 independent parts, one for each index of `groups`. A program takes and returns all parts, laid end to end along the dimension named above; an argument that names none is the same for every part. Nothing has to cross between parts.
All inputs are finite; a program needn't handle non-finite values. Where the computation divides by a largest or mean magnitude, that divisor is 1e-20 or more.
Results may differ from a plain program's by a relative error of at most 0.0095.
Values may be sent and summed in bfloat16 or wider, within the bound.
No kernel may reach another device: no remote copies, remote signals or barrier semaphores. Data moves between devices by JAX's collectives and lax.ppermute only.
A program may use at most 64 MiB of HBM per device.

v0:
```python
import functools

import jax
import jax.numpy as jnp
from jax import lax
from jax.experimental import pallas as pl
from jax.experimental.pallas import tpu as pltpu
from jax.sharding import PartitionSpec as P


EPS = 1e-05
TINY = 1e-06
TOP = 448.0
BF16, F32 = jnp.bfloat16, jnp.float32
STAT_ROWS = 8
NEAR = (1, -1, 0)
VMEM = pl.BlockSpec(memory_space=pltpu.VMEM)
SMEM = pl.BlockSpec(memory_space=pltpu.SMEM)
ANY = pl.BlockSpec(memory_space=pl.ANY)


def params(mib):
    return pltpu.CompilerParams(vmem_limit_bytes=mib << 20)


def cost(flops, moved):
    return pl.CostEstimate(flops=flops, bytes_accessed=moved, transcendentals=0)


def terms_kernel(dims, place_ref, heads_ref, weight_ref, far_sent_ref, far_mine_ref, near_sent_ref, near_mine_ref):
    tp, tq, tr, width = dims
    core, here = place_ref[0], place_ref[1]
    span = tr * width
    heads = heads_ref[...]
    for t in range(tp):
        for k, step in enumerate((tq // 2,) + NEAR):
            q = lax.rem(here + (step + tq), tq)
            columns = pl.ds(pl.multiple_of((t * tq + q) * span, span), span)
            terms = jnp.dot(heads, weight_ref[:, columns], preferred_element_type=F32)
            low, high = terms[:, 0:width], terms[:, width:span]
            mine = jnp.where(core == 0, low, high)
            sent = jnp.where(core == 0, high, low).astype(BF16)
            if k == 0:
                far_mine_ref[t] = mine
                far_sent_ref[t] = sent
            else:
                near_mine_ref[k - 1, t] = mine
                near_sent_ref[k - 1, t] = sent


def all_terms(place, heads, weight, dims):
    tp, _, _, width = dims
    tokens, _ = heads.shape
    far, near = (tp, tokens, width), (len(NEAR), tp, tokens, width)
    return pl.pallas_call(
        functools.partial(terms_kernel, dims),
        out_shape=(
            jax.ShapeDtypeStruct(far, BF16),
            jax.ShapeDtypeStruct(far, F32),
            jax.ShapeDtypeStruct(near, BF16),
            jax.ShapeDtypeStruct(near, F32),
        ),
        in_specs=[SMEM, VMEM, VMEM],
        out_specs=(VMEM,) * 4,
        compiler_params=params(16),
        cost_estimate=cost(2 * tokens * weight.size, 2 * weight.size),
        name="all_terms",
    )(place, heads, weight)


def far_kernel(mine_ref, other_ref, right_ref, left_ref):
    half = right_ref.shape[0]
    for k in range(half):
        right_ref[k] = (mine_ref[k] + other_ref[k].astype(F32)).astype(BF16)
        left_ref[k] = (mine_ref[half + k] + other_ref[half + k].astype(F32)).astype(BF16)


def far_block(mine, other):
    half = jax.ShapeDtypeStruct((mine.shape[0] // 2, *mine.shape[1:]), BF16)
    return pl.pallas_call(
        far_kernel,
        out_shape=(half, half),
        in_specs=[VMEM, VMEM],
        out_specs=(VMEM, VMEM),
        compiler_params=params(16),
        cost_estimate=cost(mine.size, 8 * mine.size),
        name="far_block",
    )(mine, other)


def near_kernel(mine_ref, other_ref, left_got_ref, right_got_ref, right_ref, left_ref, own_ref):
    half = left_got_ref.shape[0]
    for t in range(right_ref.shape[0]):
        right = mine_ref[0, t] + other_ref[0, t].astype(F32)
        left = mine_ref[1, t] + other_ref[1, t].astype(F32)
        if t < half:
            right = right + left_got_ref[t].astype(F32)
        else:
            left = left + right_got_ref[t - half].astype(F32)
        right_ref[t] = right.astype(BF16)
        left_ref[t] = left.astype(BF16)
        own_ref[t] = mine_ref[2, t] + other_ref[2, t].astype(F32)


def near_blocks(mine, other, left_got, right_got):
    shape = mine.shape[1:]
    block = jax.ShapeDtypeStruct(shape, BF16)
    return pl.pallas_call(
        near_kernel,
        out_shape=(block, block, jax.ShapeDtypeStruct(shape, F32)),
        in_specs=[VMEM] * 4,
        out_specs=(VMEM, VMEM, VMEM),
        compiler_params=params(16),
        cost_estimate=cost(mine.size, 8 * mine.size),
        name="near_blocks",
    )(mine, other, left_got, right_got)


def summed_kernel(own_ref, left_ref, right_ref, out_ref):
    for t in range(out_ref.shape[0]):
        total = own_ref[t] + left_ref[t].astype(F32) + right_ref[t].astype(F32)
        out_ref[t] = total.astype(BF16)


def summed(own, left, right):
    return pl.pallas_call(
        summed_kernel,
        out_shape=jax.ShapeDtypeStruct(own.shape, BF16),
        in_specs=[VMEM] * 3,
        out_specs=VMEM,
        compiler_params=params(16),
        cost_estimate=cost(2 * own.size, 8 * own.size),
        name="summed",
    )(own, left, right)


def in_three(value):
    first = value.astype(BF16)
    rest = value - first.astype(F32)
    second = rest.astype(BF16)
    third = (rest - second.astype(F32)).astype(BF16)
    return [first.astype(F32), second.astype(F32), third.astype(F32)]


def normed_kernel(parts_ref, residual_ref, gain_ref, hidden_ref, sent_ref):
    total = parts_ref[0].astype(F32)
    for k in range(1, parts_ref.shape[0]):
        total = total + parts_ref[k].astype(F32)
    hidden = (residual_ref[...].astype(F32) + total).astype(BF16)
    hidden_ref[...] = hidden
    widened = hidden.astype(F32)
    gained = widened * gain_ref[...].astype(F32)
    tokens, width = gained.shape
    blank = jnp.zeros((width - tokens, width), F32)

    def turned(rows):
        return jnp.transpose(jnp.concatenate([rows, blank], axis=0))

    squares = jnp.sum(turned(widened * widened), axis=0, keepdims=True)
    top = jnp.max(turned(jnp.abs(gained)), axis=0, keepdims=True)
    lines = in_three(squares) + in_three(top)
    lines.append(jnp.zeros((STAT_ROWS - len(lines), width), F32))
    block = jnp.concatenate([gained] + lines, axis=0).astype(BF16)
    for k in range(sent_ref.shape[0]):
        sent_ref[k] = block


def normed(parts, residual, gain):
    copies, tokens, width = parts.shape
    return pl.pallas_call(
        normed_kernel,
        out_shape=(
            jax.ShapeDtypeStruct((tokens, width), BF16),
            jax.ShapeDtypeStruct((copies, tokens + STAT_ROWS, width), BF16),
        ),
        in_specs=[VMEM, VMEM, VMEM],
        out_specs=(VMEM, VMEM),
        compiler_params=params(16),
        cost_estimate=cost(parts.size, 4 * parts.size),
        name="normed",
    )(parts, residual, gain)


def query_sum(core, dims, tokens, found_ref, weight_ref):
    tp, tq, tr, width = dims
    group = 4
    total = None
    for q in range(tq):
        for t in range(0, tp, group):
            turns = range(t, min(t + group, tp))
            starts = [pl.multiple_of(((k * tq + q) * tr + core) * width, width) for k in turns]
            left = jnp.concatenate(
                [found_ref[q, k * tokens : (k + 1) * tokens, :] for k in turns], axis=1
            )
            right = jnp.concatenate([weight_ref[pl.ds(at, width), :] for at in starts], axis=0)
            term = jnp.dot(left, right, preferred_element_type=F32)
            total = term if total is None else total + term
    return total


def stat_lines(blocks):
    squares, top = None, None
    for block in blocks:
        lines = block.astype(F32)
        found = (lines[0:1] + lines[1:2]) + lines[2:3]
        largest = (lines[3:4] + lines[4:5]) + lines[5:6]
        squares = found if squares is None else squares + found
        top = largest if top is None else jnp.maximum(top, largest)
    return squares, top


def plane_stats(found_ref):
    rows = found_ref.shape[1]
    return stat_lines([found_ref[q, rows - STAT_ROWS :, :] for q in range(found_ref.shape[0])])


def query_kernel(dims, features, core_ref, mine_ref, other_ref, weight_ref, query_ref, peak_ref):
    tokens, width = query_ref.shape
    core = core_ref[0]
    squares, top = plane_stats(mine_ref)
    other_squares, other_top = plane_stats(other_ref)
    squares = squares + other_squares
    top = jnp.maximum(top, other_top)
    inv_rms = lax.rsqrt(squares / features + EPS)
    peak = top * inv_rms
    peak_ref[...] = peak[:, 0:tokens]
    scale = inv_rms * (TOP / (peak + TINY)) * ((peak + TINY) / TOP)
    column = jnp.transpose(jnp.broadcast_to(scale, (width, width)))
    total = query_sum(core, dims, tokens, mine_ref, weight_ref)
    total = total + query_sum(1 - core, dims, tokens, other_ref, weight_ref)
    query_ref[...] = (total * column[0:tokens, :]).astype(BF16)


def query_all(core, mine, other, weight, dims, tokens, features):
    width = dims[3]
    return pl.pallas_call(
        functools.partial(query_kernel, dims, features),
        out_shape=(
            jax.ShapeDtypeStruct((tokens, width), BF16),
            jax.ShapeDtypeStruct((1, tokens), F32),
        ),
        in_specs=[SMEM, VMEM, VMEM, VMEM],
        out_specs=(VMEM, VMEM),
        compiler_params=params(16),
        cost_estimate=cost(2 * tokens * weight.size, 2 * weight.size),
        name="query_all",
    )(core, mine, other, weight)


def restacked_kernel(line_ref, out_ref):
    tp, rows, width = line_ref.shape
    tokens = rows - STAT_ROWS
    squares, top = stat_lines([line_ref[t, tokens:rows, :] for t in range(tp)])
    lines = in_three(squares) + in_three(top)
    lines.append(jnp.zeros((STAT_ROWS - len(lines), width), F32))
    block = jnp.concatenate(lines, axis=0).astype(BF16)
    for k in range(out_ref.shape[0]):
        for t in range(tp):
            out_ref[k, t * tokens : (t + 1) * tokens, :] = line_ref[t, 0:tokens, :]
        out_ref[k, tp * tokens : tp * tokens + STAT_ROWS, :] = block


def restacked(line, copies):
    tp, rows, width = line.shape
    shape = (copies, tp * (rows - STAT_ROWS) + STAT_ROWS, width)
    return pl.pallas_call(
        restacked_kernel,
        out_shape=jax.ShapeDtypeStruct(shape, BF16),
        in_specs=[VMEM],
        out_specs=VMEM,
        compiler_params=params(16),
        cost_estimate=cost(line.size, 8 * line.size),
        name="restacked",
    )(line)


def exchanged(blocks, axis):
    return lax.all_to_all(blocks, axis, split_axis=0, concat_axis=0, tiled=True)


def swapped(array):
    return lax.ppermute(array, "tr", [(0, 1), (1, 0)])


def moved(array, step):
    size = lax.axis_size("tq")
    return lax.ppermute(array, "tq", [(k, (k + step) % size) for k in range(size)])


def step(attn_heads, residual, o_weight, norm_gain, q_weight):
    tp, tq, tr = (lax.axis_size(axis) for axis in ("tp", "tq", "tr"))
    tokens, width = residual.shape
    features = o_weight.shape[1]
    dims = (tp, tq, tr, width)
    core = lax.axis_index("tr").astype(jnp.int32)
    here = lax.axis_index("tq").astype(jnp.int32)
    place = jnp.stack([core, here])

    far_sent, far_mine, near_sent, near_mine = all_terms(place, attn_heads, o_weight, dims)
    far_right, far_left = far_block(far_mine, swapped(far_sent))
    near_came = swapped(near_sent)
    left_got, right_got = moved(far_right, 1), moved(far_left, -1)
    right, left, own = near_blocks(near_mine, near_came, left_got, right_got)
    section = summed(own, moved(right, 1), moved(left, -1))
    hidden, block = normed(exchanged(section, "tp"), residual, norm_gain.reshape(1, width))

    plane = exchanged(restacked(exchanged(block, "tp"), tq), "tq")
    other_plane = swapped(plane)
    query, peak = query_all(
        core.reshape(1), plane, other_plane, q_weight, dims, tokens, features
    )
    return hidden, peak.reshape(tokens), query


def solution(mesh):
    split = ("tp", "tq", "tr")
    placed = (P("groups", split), P("groups", split), P(split, None), P(split), P(None, split))
    return jax.shard_map(
        step,
        mesh=mesh,
        in_specs=placed,
        out_specs=(P("groups", split), P("groups"), P("groups", split)),
        check_vma=False,
    )
```

profile of v0, /device:TPU:161, one launch (start us, length us, event | category | flops | bytes accessed | tf_op | source)
XLA Modules:
  0.0 111.3 jit_solution(5161802395043320585)
XLA Ops:
  0.6 0.1 pad_add_fusion.place_ref
  0.7 0.0 copy-start.1
  0.7 2.2 %copy-done.1 = bf16[128,16384]{1,0:T(8,128)(2,1)S(1)} copy-done((bf16[128,16384]{1,0:T(8,128)(2,1)S(1)}, bf16[128,16384]{1,0:T(8,128)(2,1)}, u32[]{:S(2)}) %copy-start.1) | copy-done | bytes 4194328
  2.9 0.0 copy-start.2
  2.9 0.7 copy-done.2
  3.6 1.3 %all_terms.1 = (bf16[16,64,128]{2,1,0:T(8,128)(2,1)S(1)}, f32[16,64,128]{2,1,0:T(8,128)S(1)}, bf16[3,16,64,128]{3,2,1,0:T(8,128)(2,1)S(1)}, f32[3,16,64,128]{3,2,1,0:T(8,128)S(1)}) custom-call(s32[2]{0:T(128)S(1)} %pad_add_fusion.place_ref, bf16[64,128]{1,0:T(8,128)(2,1)S(1)} %copy-done.2, bf16[128,16384]{1,0:T(8,128)(2,1)S(1)} %copy-done.1), custom_call_target="tpu_custom_call" | custom-call | flops 268435456 | bytes 4194304 | tf_op jit(solution)/shard_map/all_terms/pallas_call | solution.py:55
  4.9 0.7 collective-permute-start
  5.6 0.1 collective-permute-start.1
  5.8 2.1 %collective-permute-done.1.other_ref = bf16[16,64,128]{2,1,0:T(8,128)(2,1)S(1)} collective-permute-done((bf16[16,64,128]{2,1,0:T(8,128)(2,1)S(1)}, bf16[16,64,128]{2,1,0:T(8,128)(2,1)S(1)}, u32[]{:S(2)}, u32[]{:S(2)}) %collective-permute-start.1) | collective-permute-done | bytes 262176 | tf_op jit(solution)/shard_map/ppermute | solution.py:282
  7.9 0.1 far_block.1
  8.0 1.5 %collective-permute-start.2 = (bf16[8,64,128]{2,1,0:T(8,128)(2,1)S(1)}, bf16[8,64,128]{2,1,0:T(8,128)(2,1)S(1)}, u32[]{:S(2)}, u32[]{:S(2)}) collective-permute-start(bf16[8,64,128]{2,1,0:T(8,128)(2,1)S(1)} %get-tuple-element.20), channel_id=1, source_target_pairs={{0,2},{2,4},{4,6},{6,0},{1,3},{3,5},{5,7},{7,1},{8,10},{10,12},{12... | collective-permute-start | bytes 393224 | tf_op jit(solution)/shard_map/ppermute | solution.py:287
  9.4 1.7 %collective-permute-start.3 = (bf16[8,64,128]{2,1,0:T(8,128)(2,1)S(1)}, bf16[8,64,128]{2,1,0:T(8,128)(2,1)S(1)}, u32[]{:S(2)}, u32[]{:S(2)}) collective-permute-start(bf16[8,64,128]{2,1,0:T(8,128)(2,1)S(1)} %get-tuple-element.21), channel_id=1, source_target_pairs={{0,6},{2,0},{4,2},{6,4},{1,7},{3,1},{5,3},{7,5},{8,14},{10,8},{12,... | collective-permute-start | bytes 393224 | tf_op jit(solution)/shard_map/ppermute | solution.py:287
  11.1 3.3 %collective-permute-done.2.left_got_ref = bf16[8,64,128]{2,1,0:T(8,128)(2,1)S(1)} collective-permute-done((bf16[8,64,128]{2,1,0:T(8,128)(2,1)S(1)}, bf16[8,64,128]{2,1,0:T(8,128)(2,1)S(1)}, u32[]{:S(2)}, u32[]{:S(2)}) %collective-permute-start.2) | collective-permute-done | bytes 131104 | tf_op jit(solution)/shard_map/ppermute | solution.py:287
  14.4 0.0 collective-permute-done.3.right_got_ref
  14.4 0.0 collective-permute-done.other_ref
  14.4 0.2 near_blocks.1
  14.6 0.0 copy-start.3
  14.6 0.0 copy-start.4
  14.7 0.8 collective-permute-start.4
  15.5 2.0 %collective-permute-start.5 = (bf16[16,64,128]{2,1,0:T(8,128)(2,1)S(1)}, bf16[16,64,128]{2,1,0:T(8,128)(2,1)S(1)}, u32[]{:S(2)}, u32[]{:S(2)}) collective-permute-start(bf16[16,64,128]{2,1,0:T(8,128)(2,1)S(1)} %get-tuple-element.24), channel_id=1, source_target_pairs={{0,6},{2,0},{4,2},{6,4},{1,7},{3,1},{5,3},{7,5},{8,14},{10,8},{12,... | collective-permute-start | bytes 786440 | tf_op jit(solution)/shard_map/ppermute | solution.py:287
  17.5 5.4 %collective-permute-done.4.left_ref = bf16[16,64,128]{2,1,0:T(8,128)(2,1)S(1)} collective-permute-done((bf16[16,64,128]{2,1,0:T(8,128)(2,1)S(1)}, bf16[16,64,128]{2,1,0:T(8,128)(2,1)S(1)}, u32[]{:S(2)}, u32[]{:S(2)}) %collective-permute-start.4) | collective-permute-done | bytes 262176 | tf_op jit(solution)/shard_map/ppermute | solution.py:287
  22.8 0.0 collective-permute-done.5.right_ref
  22.8 0.1 summed.1
  22.9 36.9 %all_to_all.15.parts_ref = bf16[16,64,128]{2,1,0:T(8,128)(2,1)S(1)} all-to-all(bf16[16,64,128]{2,1,0:T(8,128)(2,1)S(1)} %summed.1), channel_id=1, replica_groups=mesh['groups'=2,'tp'=16,'tq'=4,'tr'=2] {'tp'}, dimensions={0} | all-to-all | bytes 524288 | tf_op jit(solution)/shard_map/all_to_all | solution.py:278
  59.9 0.0 copy-done.3
  59.9 0.0 copy-done.4
  59.9 0.0 copy-start
  59.9 0.7 normed.1
  60.5 26.3 %all_to_all.16.line_ref = bf16[16,72,128]{2,1,0:T(8,128)(2,1)S(1)} all-to-all(bf16[16,72,128]{2,1,0:T(8,128)(2,1)S(1)} %get-tuple-element.26), channel_id=1, replica_groups=mesh['groups'=2,'tp'=16,'tq'=4,'tr'=2] {'tp'}, dimensions={0} | all-to-all | bytes 589824 | tf_op jit(solution)/shard_map/all_to_all | solution.py:278
  86.8 0.1 restacked.1
  87.0 17.9 %all_to_all.17.mine_ref = bf16[4,1032,128]{2,1,0:T(8,128)(2,1)S(1)} all-to-all(bf16[4,1032,128]{2,1,0:T(8,128)(2,1)S(1)} %restacked.1), channel_id=1, replica_groups=mesh['groups'=2,'tp'=16,'tq'=4,'tr'=2] {'tq'}, dimensions={0} | all-to-all | bytes 2113536 | tf_op jit(solution)/shard_map/all_to_all | solution.py:278
  104.9 2.6 %collective-permute-start.6 = (bf16[4,1032,128]{2,1,0:T(8,128)(2,1)S(1)}, bf16[4,1032,128]{2,1,0:T(8,128)(2,1)S(1)}, u32[]{:S(2)}, u32[]{:S(2)}) collective-permute-start(bf16[4,1032,128]{2,1,0:T(8,128)(2,1)S(1)} %all_to_all.17.mine_ref), channel_id=1, source_target_pairs={{0,1},{1,0},{2,3},{3,2},{4,5},{5,4},{6,7},{7,6},{8,9},{9,8},{10,11... | collective-permute-start | bytes 3170312 | tf_op jit(solution)/shard_map/ppermute | solution.py:282
  107.5 2.3 %collective-permute-done.6.other_ref = bf16[4,1032,128]{2,1,0:T(8,128)(2,1)S(1)} collective-permute-done((bf16[4,1032,128]{2,1,0:T(8,128)(2,1)S(1)}, bf16[4,1032,128]{2,1,0:T(8,128)(2,1)S(1)}, u32[]{:S(2)}, u32[]{:S(2)}) %collective-permute-start.6) | collective-permute-done | bytes 1056800 | tf_op jit(solution)/shard_map/ppermute | solution.py:282
  109.8 0.0 copy-done
  109.8 1.6 %query_all.1 = (bf16[64,128]{1,0:T(8,128)(2,1)}, f32[1,64]{1,0:T(1,128)}) custom-call(s32[1]{0:T(128)} %bitcast.core_ref, bf16[4,1032,128]{2,1,0:T(8,128)(2,1)S(1)} %all_to_all.17.mine_ref, bf16[4,1032,128]{2,1,0:T(8,128)(2,1)S(1)} %collective-permute-done.6.other_ref, bf16[16384,128]{1,0:T(8,128)(2,1)S(1)} %copy-done), custom_call_target="tpu_custom_call" | custom-call | flops 268435456 | bytes 4194304 | tf_op jit(solution)/shard_map/query_all/pallas_call | solution.py:236
Async XLA Ops:
  0.7 2.2 %copy-start.1 = (bf16[128,16384]{1,0:T(8,128)(2,1)S(1)}, bf16[128,16384]{1,0:T(8,128)(2,1)}, u32[]{:S(2)}) copy-start(bf16[128,16384]{1,0:T(8,128)(2,1)} %weight_ref.2) | copy-start | bytes 12582916
  2.9 0.7 copy-start.2
  4.9 9.5 %collective-permute-start = (bf16[3,16,64,128]{3,2,1,0:T(8,128)(2,1)S(1)}, bf16[3,16,64,128]{3,2,1,0:T(8,128)(2,1)S(1)}, u32[]{:S(2)}, u32[]{:S(2)}) collective-permute-start(bf16[3,16,64,128]{3,2,1,0:T(8,128)(2,1)S(1)} %get-tuple-element.17), channel_id=1, source_target_pairs={{0,1},{1,0},{2,3},{3,2},{4,5},{5,4},{6,7},{7,6},{8,9},{9,8},{10,11... | collective-permute-start | bytes 2359304 | tf_op jit(solution)/shard_map/ppermute | solution.py:282
  5.6 2.3 %collective-permute-start.1 = (bf16[16,64,128]{2,1,0:T(8,128)(2,1)S(1)}, bf16[16,64,128]{2,1,0:T(8,128)(2,1)S(1)}, u32[]{:S(2)}, u32[]{:S(2)}) collective-permute-start(bf16[16,64,128]{2,1,0:T(8,128)(2,1)S(1)} %get-tuple-element.19), channel_id=1, source_target_pairs={{0,1},{1,0},{2,3},{3,2},{4,5},{5,4},{6,7},{7,6},{8,9},{9,8},{10,11... | collective-permute-start | bytes 786440 | tf_op jit(solution)/shard_map/ppermute | solution.py:282
  8.0 6.5 %collective-permute-start.2 = (bf16[8,64,128]{2,1,0:T(8,128)(2,1)S(1)}, bf16[8,64,128]{2,1,0:T(8,128)(2,1)S(1)}, u32[]{:S(2)}, u32[]{:S(2)}) collective-permute-start(bf16[8,64,128]{2,1,0:T(8,128)(2,1)S(1)} %get-tuple-element.20), channel_id=1, source_target_pairs={{0,2},{2,4},{4,6},{6,0},{1,3},{3,5},{5,7},{7,1},{8,10},{10,12},{12... | collective-permute-start | bytes 393224 | tf_op jit(solution)/shard_map/ppermute | solution.py:287
  9.4 5.0 %collective-permute-start.3 = (bf16[8,64,128]{2,1,0:T(8,128)(2,1)S(1)}, bf16[8,64,128]{2,1,0:T(8,128)(2,1)S(1)}, u32[]{:S(2)}, u32[]{:S(2)}) collective-permute-start(bf16[8,64,128]{2,1,0:T(8,128)(2,1)S(1)} %get-tuple-element.21), channel_id=1, source_target_pairs={{0,6},{2,0},{4,2},{6,4},{1,7},{3,1},{5,3},{7,5},{8,14},{10,8},{12,... | collective-permute-start | bytes 393224 | tf_op jit(solution)/shard_map/ppermute | solution.py:287
  14.6 45.2 %copy-start.3 = (bf16[64,128]{1,0:T(8,128)(2,1)S(1)}, bf16[64,128]{1,0:T(8,128)(2,1)}, u32[]{:S(2)}) copy-start(bf16[64,128]{1,0:T(8,128)(2,1)} %residual_ref.1) | copy-start | bytes 49156
  14.6 45.2 %copy-start.4 = (bf16[128]{0:T(256)(128)(2,1)S(1)}, bf16[128]{0:T(256)(128)(2,1)}, u32[]{:S(2)}) copy-start(bf16[128]{0:T(256)(128)(2,1)} %param.8) | copy-start | bytes 772
  14.7 8.2 %collective-permute-start.4 = (bf16[16,64,128]{2,1,0:T(8,128)(2,1)S(1)}, bf16[16,64,128]{2,1,0:T(8,128)(2,1)S(1)}, u32[]{:S(2)}, u32[]{:S(2)}) collective-permute-start(bf16[16,64,128]{2,1,0:T(8,128)(2,1)S(1)} %get-tuple-element.23), channel_id=1, source_target_pairs={{0,2},{2,4},{4,6},{6,0},{1,3},{3,5},{5,7},{7,1},{8,10},{10,12},{12... | collective-permute-start | bytes 786440 | tf_op jit(solution)/shard_map/ppermute | solution.py:287
  15.5 7.3 %collective-permute-start.5 = (bf16[16,64,128]{2,1,0:T(8,128)(2,1)S(1)}, bf16[16,64,128]{2,1,0:T(8,128)(2,1)S(1)}, u32[]{:S(2)}, u32[]{:S(2)}) collective-permute-start(bf16[16,64,128]{2,1,0:T(8,128)(2,1)S(1)} %get-tuple-element.24), channel_id=1, source_target_pairs={{0,6},{2,0},{4,2},{6,4},{1,7},{3,1},{5,3},{7,5},{8,14},{10,8},{12,... | collective-permute-start | bytes 786440 | tf_op jit(solution)/shard_map/ppermute | solution.py:287
  59.9 49.9 %copy-start = (bf16[16384,128]{1,0:T(8,128)(2,1)S(1)}, bf16[16384,128]{1,0:T(8,128)(2,1)}, u32[]{:S(2)}) copy-start(bf16[16384,128]{1,0:T(8,128)(2,1)} %weight_ref.3) | copy-start | bytes 12582916
  104.9 4.9 %collective-permute-start.6 = (bf16[4,1032,128]{2,1,0:T(8,128)(2,1)S(1)}, bf16[4,1032,128]{2,1,0:T(8,128)(2,1)S(1)}, u32[]{:S(2)}, u32[]{:S(2)}) collective-permute-start(bf16[4,1032,128]{2,1,0:T(8,128)(2,1)S(1)} %all_to_all.17.mine_ref), channel_id=1, source_target_pairs={{0,1},{1,0},{2,3},{3,2},{4,5},{5,4},{6,7},{7,6},{8,9},{9,8},{10,11... | collective-permute-start | bytes 3170312 | tf_op jit(solution)/shard_map/ppermute | solution.py:282
where the time goes:
time: 112 us; the launch traced here: 111 us
  blocking collectives  81.1 us (72%)
  waiting for transfers between devices  13.1 us (12%)
  starting transfers between devices  9.41 us (8%)
  Pallas kernels  3.94 us (4%)
  local copies, waits for them, and re-layouts  2.92 us (3%)
    all_to_all x3, blocking collectives, exchanged(): return lax.all_to_all(blocks, axis, split_axis=0, concat_axis=0, tiled=True)  81.1 us
    ppermute x4, waiting for transfers between devices, moved(): lax.ppermute(array, 'tq', [(k, (k + step) % size) for k in range(size)])  8.69 us
    ppermute x4, starting transfers between devices, moved(): lax.ppermute(array, 'tq', [(k, (k + step) % size) for k in range(size)])  5.96 us
    ppermute x3, waiting for transfers between devices, swapped(): return lax.ppermute(array, 'tr', [(0, 1), (1, 0)])  4.44 us
    ppermute x3, starting transfers between devices, swapped(): return lax.ppermute(array, 'tr', [(0, 1), (1, 0)])  3.45 us
    unnamed x10, local copies, waits for them, and re-layouts  2.92 us
  transfers between devices with their start and end apart: 7, of which 4 were waited for; matrix products, arithmetic and copies ran while one was open for 0% of the time, Pallas kernels for 0%

commit v1 on v0

--- a/solution.py
+++ b/solution.py
@@ -214,8 +214,9 @@
     return stat_lines([found_ref[q, rows - STAT_ROWS :, :] for q in range(found_ref.shape[0])])
 
 
-def query_kernel(dims, features, core_ref, mine_ref, other_ref, weight_ref, query_ref, peak_ref):
+def query_kernel(dims, features, core_ref, mine_ref, other_ref, weight_ref, hidden_ref, query_ref, peak_ref, hidden_out_ref):
     tokens, width = query_ref.shape
+    hidden_out_ref[...] = hidden_ref[...]
     core = core_ref[0]
     squares, top = plane_stats(mine_ref)
     other_squares, other_top = plane_stats(other_ref)
@@ -231,20 +232,21 @@
     query_ref[...] = (total * column[0:tokens, :]).astype(BF16)
 
 
-def query_all(core, mine, other, weight, dims, tokens, features):
-    width = dims[3]
+def query_all(core, mine, other, weight, hidden, dims, features):
+    tokens, width = hidden.shape
     return pl.pallas_call(
         functools.partial(query_kernel, dims, features),
         out_shape=(
             jax.ShapeDtypeStruct((tokens, width), BF16),
             jax.ShapeDtypeStruct((1, tokens), F32),
+            jax.ShapeDtypeStruct((tokens, width), BF16),
         ),
-        in_specs=[SMEM, VMEM, VMEM, VMEM],
-        out_specs=(VMEM, VMEM),
+        in_specs=[SMEM, VMEM, VMEM, VMEM, VMEM],
+        out_specs=(VMEM, VMEM, VMEM),
         compiler_params=params(16),
         cost_estimate=cost(2 * tokens * weight.size, 2 * weight.size),
         name="query_all",
-    )(core, mine, other, weight)
+    )(core, mine, other, weight, hidden)
 
 
 def restacked_kernel(line_ref, out_ref):
@@ -306,8 +308,8 @@
 
     plane = exchanged(restacked(exchanged(block, "tp"), tq), "tq")
     other_plane = swapped(plane)
-    query, peak = query_all(
-        core.reshape(1), plane, other_plane, q_weight, dims, tokens, features
+    query, peak, hidden = query_all(
+        core.reshape(1), plane, other_plane, q_weight, hidden, dims, features
     )
     return hidden, peak.reshape(tokens), query
 

time: 112 us -> 111 us (level)
  the two profiles are of different devices: /device:TPU:161 before, /device:TPU:169 now
where the time goes in v1:
time: 111 us
  blocking collectives  81.3 us (73%)
  waiting for transfers between devices  13.1 us (12%)
  starting transfers between devices  9.41 us (8%)
  Pallas kernels  3.46 us (3%)
  local copies, waits for them, and re-layouts  2.92 us (3%)
    all_to_all x3, blocking collectives, exchanged(): return lax.all_to_all(blocks, axis, split_axis=0, concat_axis=0, tiled=True)  81.3 us
    ppermute x4, waiting for transfers between devices, moved(): lax.ppermute(array, 'tq', [(k, (k + step) % size) for k in range(size)])  8.67 us
    ppermute x4, starting transfers between devices, moved(): lax.ppermute(array, 'tq', [(k, (k + step) % size) for k in range(size)])  5.96 us
    ppermute x3, waiting for transfers between devices, swapped(): return lax.ppermute(array, 'tr', [(0, 1), (1, 0)])  4.44 us
    ppermute x3, starting transfers between devices, swapped(): return lax.ppermute(array, 'tr', [(0, 1), (1, 0)])  3.45 us
    unnamed x10, local copies, waits for them, and re-layouts  2.92 us
  transfers between devices with their start and end apart: 7, of which 4 were waited for; matrix products, arithmetic and copies ran while one was open for 0% of the time, Pallas kernels for 0%

profile of v1, /device:TPU:169, one launch (start us, length us, event | category | flops | bytes accessed | tf_op | source)
XLA Modules:
  0.0 111.0 jit_solution(9717926860976428777)
XLA Ops:
  0.6 0.1 pad_add_fusion.place_ref
  0.7 0.0 copy-start.1
  0.7 2.2 %copy-done.1 = bf16[128,16384]{1,0:T(8,128)(2,1)S(1)} copy-done((bf16[128,16384]{1,0:T(8,128)(2,1)S(1)}, bf16[128,16384]{1,0:T(8,128)(2,1)}, u32[]{:S(2)}) %copy-start.1) | copy-done | bytes 4194328
  2.9 0.0 copy-start.2
  2.9 0.7 copy-done.2
  3.6 1.3 %all_terms.1 = (bf16[16,64,128]{2,1,0:T(8,128)(2,1)S(1)}, f32[16,64,128]{2,1,0:T(8,128)S(1)}, bf16[3,16,64,128]{3,2,1,0:T(8,128)(2,1)S(1)}, f32[3,16,64,128]{3,2,1,0:T(8,128)S(1)}) custom-call(s32[2]{0:T(128)S(1)} %pad_add_fusion.place_ref, bf16[64,128]{1,0:T(8,128)(2,1)S(1)} %copy-done.2, bf16[128,16384]{1,0:T(8,128)(2,1)S(1)} %copy-done.1), custom_call_target="tpu_custom_call" | custom-call | flops 268435456 | bytes 4194304 | tf_op jit(solution)/shard_map/all_terms/pallas_call | solution.py:55
  4.9 0.7 collective-permute-start
  5.6 0.1 collective-permute-start.1
  5.8 2.1 %collective-permute-done.1.other_ref = bf16[16,64,128]{2,1,0:T(8,128)(2,1)S(1)} collective-permute-done((bf16[16,64,128]{2,1,0:T(8,128)(2,1)S(1)}, bf16[16,64,128]{2,1,0:T(8,128)(2,1)S(1)}, u32[]{:S(2)}, u32[]{:S(2)}) %collective-permute-start.1) | collective-permute-done | bytes 262176 | tf_op jit(solution)/shard_map/ppermute | solution.py:284
  7.9 0.1 far_block.1
  8.0 1.5 %collective-permute-start.2 = (bf16[8,64,128]{2,1,0:T(8,128)(2,1)S(1)}, bf16[8,64,128]{2,1,0:T(8,128)(2,1)S(1)}, u32[]{:S(2)}, u32[]{:S(2)}) collective-permute-start(bf16[8,64,128]{2,1,0:T(8,128)(2,1)S(1)} %get-tuple-element.21), channel_id=1, source_target_pairs={{0,2},{2,4},{4,6},{6,0},{1,3},{3,5},{5,7},{7,1},{8,10},{10,12},{12... | collective-permute-start | bytes 393224 | tf_op jit(solution)/shard_map/ppermute | solution.py:289
  9.4 1.7 %collective-permute-start.3 = (bf16[8,64,128]{2,1,0:T(8,128)(2,1)S(1)}, bf16[8,64,128]{2,1,0:T(8,128)(2,1)S(1)}, u32[]{:S(2)}, u32[]{:S(2)}) collective-permute-start(bf16[8,64,128]{2,1,0:T(8,128)(2,1)S(1)} %get-tuple-element.22), channel_id=1, source_target_pairs={{0,6},{2,0},{4,2},{6,4},{1,7},{3,1},{5,3},{7,5},{8,14},{10,8},{12,... | collective-permute-start | bytes 393224 | tf_op jit(solution)/shard_map/ppermute | solution.py:289
  11.1 3.3 %collective-permute-done.2.left_got_ref = bf16[8,64,128]{2,1,0:T(8,128)(2,1)S(1)} collective-permute-done((bf16[8,64,128]{2,1,0:T(8,128)(2,1)S(1)}, bf16[8,64,128]{2,1,0:T(8,128)(2,1)S(1)}, u32[]{:S(2)}, u32[]{:S(2)}) %collective-permute-start.2) | collective-permute-done | bytes 131104 | tf_op jit(solution)/shard_map/ppermute | solution.py:289
  14.4 0.0 collective-permute-done.3.right_got_ref
  14.4 0.0 collective-permute-done.other_ref
  14.4 0.2 near_blocks.1
  14.6 0.0 copy-start.3
  14.6 0.0 copy-start.4
  14.6 0.9 collective-permute-start.4
  15.5 2.0 %collective-permute-start.5 = (bf16[16,64,128]{2,1,0:T(8,128)(2,1)S(1)}, bf16[16,64,128]{2,1,0:T(8,128)(2,1)S(1)}, u32[]{:S(2)}, u32[]{:S(2)}) collective-permute-start(bf16[16,64,128]{2,1,0:T(8,128)(2,1)S(1)} %get-tuple-element.25), channel_id=1, source_target_pairs={{0,6},{2,0},{4,2},{6,4},{1,7},{3,1},{5,3},{7,5},{8,14},{10,8},{12,... | collective-permute-start | bytes 786440 | tf_op jit(solution)/shard_map/ppermute | solution.py:289
  17.5 5.4 %collective-permute-done.4.left_ref = bf16[16,64,128]{2,1,0:T(8,128)(2,1)S(1)} collective-permute-done((bf16[16,64,128]{2,1,0:T(8,128)(2,1)S(1)}, bf16[16,64,128]{2,1,0:T(8,128)(2,1)S(1)}, u32[]{:S(2)}, u32[]{:S(2)}) %collective-permute-start.4) | collective-permute-done | bytes 262176 | tf_op jit(solution)/shard_map/ppermute | solution.py:289
  22.8 0.0 collective-permute-done.5.right_ref
  22.8 0.1 summed.1
  22.9 36.9 %all_to_all.15.parts_ref = bf16[16,64,128]{2,1,0:T(8,128)(2,1)S(1)} all-to-all(bf16[16,64,128]{2,1,0:T(8,128)(2,1)S(1)} %summed.1), channel_id=1, replica_groups=mesh['groups'=2,'tp'=16,'tq'=4,'tr'=2] {'tp'}, dimensions={0} | all-to-all | bytes 524288 | tf_op jit(solution)/shard_map/all_to_all | solution.py:280
  59.8 0.0 copy-done.3
  59.8 0.0 copy-done.4
  59.9 0.0 copy-start
  59.9 0.2 normed.1
  60.0 26.5 %all_to_all.16.line_ref = bf16[16,72,128]{2,1,0:T(8,128)(2,1)S(1)} all-to-all(bf16[16,72,128]{2,1,0:T(8,128)(2,1)S(1)} %get-tuple-element.26), channel_id=1, replica_groups=mesh['groups'=2,'tp'=16,'tq'=4,'tr'=2] {'tp'}, dimensions={0} | all-to-all | bytes 589824 | tf_op jit(solution)/shard_map/all_to_all | solution.py:280
  86.5 0.1 restacked.1
  86.6 17.9 %all_to_all.17.mine_ref = bf16[4,1032,128]{2,1,0:T(8,128)(2,1)S(1)} all-to-all(bf16[4,1032,128]{2,1,0:T(8,128)(2,1)S(1)} %restacked.1), channel_id=1, replica_groups=mesh['groups'=2,'tp'=16,'tq'=4,'tr'=2] {'tq'}, dimensions={0} | all-to-all | bytes 2113536 | tf_op jit(solution)/shard_map/all_to_all | solution.py:280
  104.5 2.6 %collective-permute-start.6 = (bf16[4,1032,128]{2,1,0:T(8,128)(2,1)S(1)}, bf16[4,1032,128]{2,1,0:T(8,128)(2,1)S(1)}, u32[]{:S(2)}, u32[]{:S(2)}) collective-permute-start(bf16[4,1032,128]{2,1,0:T(8,128)(2,1)S(1)} %all_to_all.17.mine_ref), channel_id=1, source_target_pairs={{0,1},{1,0},{2,3},{3,2},{4,5},{5,4},{6,7},{7,6},{8,9},{9,8},{10,11... | collective-permute-start | bytes 3170312 | tf_op jit(solution)/shard_map/ppermute | solution.py:284
  107.1 2.3 %collective-permute-done.6.other_ref = bf16[4,1032,128]{2,1,0:T(8,128)(2,1)S(1)} collective-permute-done((bf16[4,1032,128]{2,1,0:T(8,128)(2,1)S(1)}, bf16[4,1032,128]{2,1,0:T(8,128)(2,1)S(1)}, u32[]{:S(2)}, u32[]{:S(2)}) %collective-permute-start.6) | collective-permute-done | bytes 1056800 | tf_op jit(solution)/shard_map/ppermute | solution.py:284
  109.4 0.0 copy-done
  109.4 1.6 %query_all.1 = (bf16[64,128]{1,0:T(8,128)(2,1)}, f32[1,64]{1,0:T(1,128)}, bf16[64,128]{1,0:T(8,128)(2,1)}) custom-call(s32[1]{0:T(128)} %bitcast.core_ref, bf16[4,1032,128]{2,1,0:T(8,128)(2,1)S(1)} %all_to_all.17.mine_ref, bf16[4,1032,128]{2,1,0:T(8,128)(2,1)S(1)} %collective-permute-done.6.other_ref, bf16[16384,128]{1,0:T(8,128)(2,1)S(1)} %copy-done, ...), custom_call_target="tpu_custom_call" | custom-call | flops 268435456 | bytes 4194304 | tf_op jit(solution)/shard_map/query_all/pallas_call | solution.py:237
Async XLA Ops:
  0.7 2.2 %copy-start.1 = (bf16[128,16384]{1,0:T(8,128)(2,1)S(1)}, bf16[128,16384]{1,0:T(8,128)(2,1)}, u32[]{:S(2)}) copy-start(bf16[128,16384]{1,0:T(8,128)(2,1)} %weight_ref.2) | copy-start | bytes 12582916
  2.9 0.7 copy-start.2
  4.9 9.5 %collective-permute-start = (bf16[3,16,64,128]{3,2,1,0:T(8,128)(2,1)S(1)}, bf16[3,16,64,128]{3,2,1,0:T(8,128)(2,1)S(1)}, u32[]{:S(2)}, u32[]{:S(2)}) collective-permute-start(bf16[3,16,64,128]{3,2,1,0:T(8,128)(2,1)S(1)} %get-tuple-element.18), channel_id=1, source_target_pairs={{0,1},{1,0},{2,3},{3,2},{4,5},{5,4},{6,7},{7,6},{8,9},{9,8},{10,11... | collective-permute-start | bytes 2359304 | tf_op jit(solution)/shard_map/ppermute | solution.py:284
  5.6 2.3 %collective-permute-start.1 = (bf16[16,64,128]{2,1,0:T(8,128)(2,1)S(1)}, bf16[16,64,128]{2,1,0:T(8,128)(2,1)S(1)}, u32[]{:S(2)}, u32[]{:S(2)}) collective-permute-start(bf16[16,64,128]{2,1,0:T(8,128)(2,1)S(1)} %get-tuple-element.20), channel_id=1, source_target_pairs={{0,1},{1,0},{2,3},{3,2},{4,5},{5,4},{6,7},{7,6},{8,9},{9,8},{10,11... | collective-permute-start | bytes 786440 | tf_op jit(solution)/shard_map/ppermute | solution.py:284
  8.0 6.4 %collective-permute-start.2 = (bf16[8,64,128]{2,1,0:T(8,128)(2,1)S(1)}, bf16[8,64,128]{2,1,0:T(8,128)(2,1)S(1)}, u32[]{:S(2)}, u32[]{:S(2)}) collective-permute-start(bf16[8,64,128]{2,1,0:T(8,128)(2,1)S(1)} %get-tuple-element.21), channel_id=1, source_target_pairs={{0,2},{2,4},{4,6},{6,0},{1,3},{3,5},{5,7},{7,1},{8,10},{10,12},{12... | collective-permute-start | bytes 393224 | tf_op jit(solution)/shard_map/ppermute | solution.py:289
  9.4 5.0 %collective-permute-start.3 = (bf16[8,64,128]{2,1,0:T(8,128)(2,1)S(1)}, bf16[8,64,128]{2,1,0:T(8,128)(2,1)S(1)}, u32[]{:S(2)}, u32[]{:S(2)}) collective-permute-start(bf16[8,64,128]{2,1,0:T(8,128)(2,1)S(1)} %get-tuple-element.22), channel_id=1, source_target_pairs={{0,6},{2,0},{4,2},{6,4},{1,7},{3,1},{5,3},{7,5},{8,14},{10,8},{12,... | collective-permute-start | bytes 393224 | tf_op jit(solution)/shard_map/ppermute | solution.py:289
  14.6 45.2 %copy-start.3 = (bf16[64,128]{1,0:T(8,128)(2,1)S(1)}, bf16[64,128]{1,0:T(8,128)(2,1)}, u32[]{:S(2)}) copy-start(bf16[64,128]{1,0:T(8,128)(2,1)} %residual_ref.1) | copy-start | bytes 49156
  14.6 45.2 %copy-start.4 = (bf16[128]{0:T(256)(128)(2,1)S(1)}, bf16[128]{0:T(256)(128)(2,1)}, u32[]{:S(2)}) copy-start(bf16[128]{0:T(256)(128)(2,1)} %param.8) | copy-start | bytes 772
  14.6 8.2 %collective-permute-start.4 = (bf16[16,64,128]{2,1,0:T(8,128)(2,1)S(1)}, bf16[16,64,128]{2,1,0:T(8,128)(2,1)S(1)}, u32[]{:S(2)}, u32[]{:S(2)}) collective-permute-start(bf16[16,64,128]{2,1,0:T(8,128)(2,1)S(1)} %get-tuple-element.24), channel_id=1, source_target_pairs={{0,2},{2,4},{4,6},{6,0},{1,3},{3,5},{5,7},{7,1},{8,10},{10,12},{12... | collective-permute-start | bytes 786440 | tf_op jit(solution)/shard_map/ppermute | solution.py:289
  15.5 7.3 %collective-permute-start.5 = (bf16[16,64,128]{2,1,0:T(8,128)(2,1)S(1)}, bf16[16,64,128]{2,1,0:T(8,128)(2,1)S(1)}, u32[]{:S(2)}, u32[]{:S(2)}) collective-permute-start(bf16[16,64,128]{2,1,0:T(8,128)(2,1)S(1)} %get-tuple-element.25), channel_id=1, source_target_pairs={{0,6},{2,0},{4,2},{6,4},{1,7},{3,1},{5,3},{7,5},{8,14},{10,8},{12,... | collective-permute-start | bytes 786440 | tf_op jit(solution)/shard_map/ppermute | solution.py:289
  59.9 49.6 %copy-start = (bf16[16384,128]{1,0:T(8,128)(2,1)S(1)}, bf16[16384,128]{1,0:T(8,128)(2,1)}, u32[]{:S(2)}) copy-start(bf16[16384,128]{1,0:T(8,128)(2,1)} %weight_ref.3) | copy-start | bytes 12582916
  104.5 4.9 %collective-permute-start.6 = (bf16[4,1032,128]{2,1,0:T(8,128)(2,1)S(1)}, bf16[4,1032,128]{2,1,0:T(8,128)(2,1)S(1)}, u32[]{:S(2)}, u32[]{:S(2)}) collective-permute-start(bf16[4,1032,128]{2,1,0:T(8,128)(2,1)S(1)} %all_to_all.17.mine_ref), channel_id=1, source_target_pairs={{0,1},{1,0},{2,3},{3,2},{4,5},{5,4},{6,7},{7,6},{8,9},{9,8},{10,11... | collective-permute-start | bytes 3170312 | tf_op jit(solution)/shard_map/ppermute | solution.py:284

commit v2 on v1

--- a/solution.py
+++ b/solution.py
@@ -214,25 +214,46 @@
     return stat_lines([found_ref[q, rows - STAT_ROWS :, :] for q in range(found_ref.shape[0])])
 
 
-def query_kernel(dims, features, core_ref, mine_ref, other_ref, weight_ref, hidden_ref, query_ref, peak_ref, hidden_out_ref):
+def query_half_kernel(dims, core_ref, found_ref, weight_ref, part_ref, stat_ref):
+    tokens = part_ref.shape[0]
+    part_ref[...] = query_sum(core_ref[0], dims, tokens, found_ref, weight_ref)
+    squares, top = plane_stats(found_ref)
+    stat_ref[0:1, :] = squares
+    stat_ref[1:2, :] = top
+
+
+def query_half(core, found, weight, dims, tokens):
+    width = dims[3]
+    return pl.pallas_call(
+        functools.partial(query_half_kernel, dims),
+        out_shape=(
+            jax.ShapeDtypeStruct((tokens, width), F32),
+            jax.ShapeDtypeStruct((2, width), F32),
+        ),
+        in_specs=[SMEM, VMEM, VMEM],
+        out_specs=(VMEM, VMEM),
+        compiler_params=params(16),
+        cost_estimate=cost(tokens * weight.size, weight.size),
+        name="query_half",
+    )(core, found, weight)
+
+
+def query_kernel(dims, features, core_ref, part_ref, stat_ref, other_ref, weight_ref, hidden_ref, query_ref, peak_ref, hidden_out_ref):
     tokens, width = query_ref.shape
     hidden_out_ref[...] = hidden_ref[...]
-    core = core_ref[0]
-    squares, top = plane_stats(mine_ref)
-    other_squares, other_top = plane_stats(other_ref)
-    squares = squares + other_squares
-    top = jnp.maximum(top, other_top)
+    squares, top = plane_stats(other_ref)
+    squares = squares + stat_ref[0:1, :]
+    top = jnp.maximum(top, stat_ref[1:2, :])
     inv_rms = lax.rsqrt(squares / features + EPS)
     peak = top * inv_rms
     peak_ref[...] = peak[:, 0:tokens]
     scale = inv_rms * (TOP / (peak + TINY)) * ((peak + TINY) / TOP)
     column = jnp.transpose(jnp.broadcast_to(scale, (width, width)))
-    total = query_sum(core, dims, tokens, mine_ref, weight_ref)
-    total = total + query_sum(1 - core, dims, tokens, other_ref, weight_ref)
-    query_ref[...] = (total * column[0:tokens, :]).astype(BF16)
-
-
-def query_all(core, mine, other, weight, hidden, dims, features):
+    other = query_sum(1 - core_ref[0], dims, tokens, other_ref, weight_ref)
+    query_ref[...] = ((part_ref[...] + other) * column[0:tokens, :]).astype(BF16)
+
+
+def query_rest(core, part, stats, other, weight, hidden, dims, features):
     tokens, width = hidden.shape
     return pl.pallas_call(
         functools.partial(query_kernel, dims, features),
@@ -241,12 +262,12 @@
             jax.ShapeDtypeStruct((1, tokens), F32),
             jax.ShapeDtypeStruct((tokens, width), BF16),
         ),
-        in_specs=[SMEM, VMEM, VMEM, VMEM, VMEM],
+        in_specs=[SMEM] + [VMEM] * 5,
         out_specs=(VMEM, VMEM, VMEM),
         compiler_params=params(16),
-        cost_estimate=cost(2 * tokens * weight.size, 2 * weight.size),
-        name="query_all",
-    )(core, mine, other, weight, hidden)
+        cost_estimate=cost(tokens * weight.size, weight.size),
+        name="query_rest",
+    )(core, part, stats, other, weight, hidden)
 
 
 def restacked_kernel(line_ref, out_ref):
@@ -308,8 +329,10 @@
 
     plane = exchanged(restacked(exchanged(block, "tp"), tq), "tq")
     other_plane = swapped(plane)
-    query, peak, hidden = query_all(
-        core.reshape(1), plane, other_plane, q_weight, hidden, dims, features
+    mine_core = core.reshape(1)
+    part, stats = query_half(mine_core, plane, q_weight, dims, tokens)
+    query, peak, hidden = query_rest(
+        mine_core, part, stats, other_plane, q_weight, hidden, dims, features
     )
     return hidden, peak.reshape(tokens), query
 

time: 111 us -> 111 us (level)
  the two profiles are of different devices: /device:TPU:169 before, /device:TPU:161 now
where the time goes in v2:
time: 111 us
  blocking collectives  81.3 us (73%)
  waiting for transfers between devices  12.6 us (11%)
  starting transfers between devices  9.41 us (8%)
  Pallas kernels  3.59 us (3%)
  local copies, waits for them, and re-layouts  2.92 us (3%)
    all_to_all x3, blocking collectives, exchanged(): return lax.all_to_all(blocks, axis, split_axis=0, concat_axis=0, tiled=True)  81.3 us
    ppermute x4, waiting for transfers between devices, moved(): lax.ppermute(array, 'tq', [(k, (k + step) % size) for k in range(size)])  8.69 us
    ppermute x4, starting transfers between devices, moved(): lax.ppermute(array, 'tq', [(k, (k + step) % size) for k in range(size)])  5.96 us
    ppermute x3, waiting for transfers between devices, swapped(): return lax.ppermute(array, 'tr', [(0, 1), (1, 0)])  3.9 us
    ppermute x3, starting transfers between devices, swapped(): return lax.ppermute(array, 'tr', [(0, 1), (1, 0)])  3.45 us
    unnamed x10, local copies, waits for them, and re-layouts  2.92 us
  transfers between devices with their start and end apart: 7, of which 4 were waited for; matrix products, arithmetic and copies ran while one was open for 0% of the time, Pallas kernels for 1%

profile of v2, /device:TPU:161, one launch (start us, length us, event | category | flops | bytes accessed | tf_op | source)
XLA Modules:
  0.0 110.6 jit_solution(6585223904196444331)
XLA Ops:
  0.6 0.1 pad_add_fusion.place_ref
  0.7 0.0 copy-start.1
  0.7 2.2 %copy-done.1 = bf16[128,16384]{1,0:T(8,128)(2,1)S(1)} copy-done((bf16[128,16384]{1,0:T(8,128)(2,1)S(1)}, bf16[128,16384]{1,0:T(8,128)(2,1)}, u32[]{:S(2)}) %copy-start.1) | copy-done | bytes 4194328
  2.9 0.0 copy-start.2
  2.9 0.7 copy-done.2
  3.6 1.3 %all_terms.1 = (bf16[16,64,128]{2,1,0:T(8,128)(2,1)S(1)}, f32[16,64,128]{2,1,0:T(8,128)S(1)}, bf16[3,16,64,128]{3,2,1,0:T(8,128)(2,1)S(1)}, f32[3,16,64,128]{3,2,1,0:T(8,128)S(1)}) custom-call(s32[2]{0:T(128)S(1)} %pad_add_fusion.place_ref, bf16[64,128]{1,0:T(8,128)(2,1)S(1)} %copy-done.2, bf16[128,16384]{1,0:T(8,128)(2,1)S(1)} %copy-done.1), custom_call_target="tpu_custom_call" | custom-call | flops 268435456 | bytes 4194304 | tf_op jit(solution)/shard_map/all_terms/pallas_call | solution.py:55
  4.9 0.7 collective-permute-start
  5.6 0.1 collective-permute-start.1
  5.8 2.1 %collective-permute-done.1.other_ref = bf16[16,64,128]{2,1,0:T(8,128)(2,1)S(1)} collective-permute-done((bf16[16,64,128]{2,1,0:T(8,128)(2,1)S(1)}, bf16[16,64,128]{2,1,0:T(8,128)(2,1)S(1)}, u32[]{:S(2)}, u32[]{:S(2)}) %collective-permute-start.1) | collective-permute-done | bytes 262176 | tf_op jit(solution)/shard_map/ppermute | solution.py:305
  7.9 0.1 far_block.1
  8.0 1.5 %collective-permute-start.2 = (bf16[8,64,128]{2,1,0:T(8,128)(2,1)S(1)}, bf16[8,64,128]{2,1,0:T(8,128)(2,1)S(1)}, u32[]{:S(2)}, u32[]{:S(2)}) collective-permute-start(bf16[8,64,128]{2,1,0:T(8,128)(2,1)S(1)} %get-tuple-element.23), channel_id=1, source_target_pairs={{0,2},{2,4},{4,6},{6,0},{1,3},{3,5},{5,7},{7,1},{8,10},{10,12},{12... | collective-permute-start | bytes 393224 | tf_op jit(solution)/shard_map/ppermute | solution.py:310
  9.4 1.7 %collective-permute-start.3 = (bf16[8,64,128]{2,1,0:T(8,128)(2,1)S(1)}, bf16[8,64,128]{2,1,0:T(8,128)(2,1)S(1)}, u32[]{:S(2)}, u32[]{:S(2)}) collective-permute-start(bf16[8,64,128]{2,1,0:T(8,128)(2,1)S(1)} %get-tuple-element.24), channel_id=1, source_target_pairs={{0,6},{2,0},{4,2},{6,4},{1,7},{3,1},{5,3},{7,5},{8,14},{10,8},{12,... | collective-permute-start | bytes 393224 | tf_op jit(solution)/shard_map/ppermute | solution.py:310
  11.1 3.3 %collective-permute-done.2.left_got_ref = bf16[8,64,128]{2,1,0:T(8,128)(2,1)S(1)} collective-permute-done((bf16[8,64,128]{2,1,0:T(8,128)(2,1)S(1)}, bf16[8,64,128]{2,1,0:T(8,128)(2,1)S(1)}, u32[]{:S(2)}, u32[]{:S(2)}) %collective-permute-start.2) | collective-permute-done | bytes 131104 | tf_op jit(solution)/shard_map/ppermute | solution.py:310
  14.4 0.0 collective-permute-done.3.right_got_ref
  14.4 0.0 collective-permute-done.other_ref
  14.4 0.2 near_blocks.1
  14.6 0.0 copy-start.3
  14.6 0.0 copy-start.4
  14.7 0.8 collective-permute-start.4
  15.5 2.0 %collective-permute-start.5 = (bf16[16,64,128]{2,1,0:T(8,128)(2,1)S(1)}, bf16[16,64,128]{2,1,0:T(8,128)(2,1)S(1)}, u32[]{:S(2)}, u32[]{:S(2)}) collective-permute-start(bf16[16,64,128]{2,1,0:T(8,128)(2,1)S(1)} %get-tuple-element.27), channel_id=1, source_target_pairs={{0,6},{2,0},{4,2},{6,4},{1,7},{3,1},{5,3},{7,5},{8,14},{10,8},{12,... | collective-permute-start | bytes 786440 | tf_op jit(solution)/shard_map/ppermute | solution.py:310
  17.5 5.4 %collective-permute-done.4.left_ref = bf16[16,64,128]{2,1,0:T(8,128)(2,1)S(1)} collective-permute-done((bf16[16,64,128]{2,1,0:T(8,128)(2,1)S(1)}, bf16[16,64,128]{2,1,0:T(8,128)(2,1)S(1)}, u32[]{:S(2)}, u32[]{:S(2)}) %collective-permute-start.4) | collective-permute-done | bytes 262176 | tf_op jit(solution)/shard_map/ppermute | solution.py:310
  22.8 0.0 collective-permute-done.5.right_ref
  22.8 0.1 summed.1
  22.9 36.9 %all_to_all.15.parts_ref = bf16[16,64,128]{2,1,0:T(8,128)(2,1)S(1)} all-to-all(bf16[16,64,128]{2,1,0:T(8,128)(2,1)S(1)} %summed.1), channel_id=1, replica_groups=mesh['groups'=2,'tp'=16,'tq'=4,'tr'=2] {'tp'}, dimensions={0} | all-to-all | bytes 524288 | tf_op jit(solution)/shard_map/all_to_all | solution.py:301
  59.9 0.0 copy-done.3
  59.9 0.0 copy-done.4
  59.9 0.0 copy-start
  59.9 0.2 normed.1
  60.0 26.5 %all_to_all.16.line_ref = bf16[16,72,128]{2,1,0:T(8,128)(2,1)S(1)} all-to-all(bf16[16,72,128]{2,1,0:T(8,128)(2,1)S(1)} %get-tuple-element.28), channel_id=1, replica_groups=mesh['groups'=2,'tp'=16,'tq'=4,'tr'=2] {'tp'}, dimensions={0} | all-to-all | bytes 589824 | tf_op jit(solution)/shard_map/all_to_all | solution.py:301
  86.5 0.1 restacked.1
  86.6 17.9 %all_to_all.17.found_ref = bf16[4,1032,128]{2,1,0:T(8,128)(2,1)S(1)} all-to-all(bf16[4,1032,128]{2,1,0:T(8,128)(2,1)S(1)} %restacked.1), channel_id=1, replica_groups=mesh['groups'=2,'tp'=16,'tq'=4,'tr'=2] {'tq'}, dimensions={0} | all-to-all | bytes 2113536 | tf_op jit(solution)/shard_map/all_to_all | solution.py:301
  104.5 2.6 %collective-permute-start.6 = (bf16[4,1032,128]{2,1,0:T(8,128)(2,1)S(1)}, bf16[4,1032,128]{2,1,0:T(8,128)(2,1)S(1)}, u32[]{:S(2)}, u32[]{:S(2)}) collective-permute-start(bf16[4,1032,128]{2,1,0:T(8,128)(2,1)S(1)} %all_to_all.17.found_ref), channel_id=1, source_target_pairs={{0,1},{1,0},{2,3},{3,2},{4,5},{5,4},{6,7},{7,6},{8,9},{9,8},{10,11... | collective-permute-start | bytes 3170312 | tf_op jit(solution)/shard_map/ppermute | solution.py:305
  107.1 0.0 copy-done
  107.1 0.5 query_half.1
  107.7 1.8 %collective-permute-done.6.other_ref = bf16[4,1032,128]{2,1,0:T(8,128)(2,1)S(1)} collective-permute-done((bf16[4,1032,128]{2,1,0:T(8,128)(2,1)S(1)}, bf16[4,1032,128]{2,1,0:T(8,128)(2,1)S(1)}, u32[]{:S(2)}, u32[]{:S(2)}) %collective-permute-start.6) | collective-permute-done | bytes 1056800 | tf_op jit(solution)/shard_map/ppermute | solution.py:305
  109.4 1.2 %query_rest.1 = (bf16[64,128]{1,0:T(8,128)(2,1)}, f32[1,64]{1,0:T(1,128)}, bf16[64,128]{1,0:T(8,128)(2,1)}) custom-call(s32[1]{0:T(128)} %bitcast.core_ref, f32[64,128]{1,0:T(8,128)S(1)} %get-tuple-element.29.part_ref, f32[2,128]{1,0:T(2,128)S(1)} %get-tuple-element.30.stat_ref, bf16[4,1032,128]{2,1,0:T(8,128)(2,1)S(1)} %collective-permute-done.6.other_ref, ...), custom_call_target="tpu_custom_call" | custom-call | flops 134217728 | bytes 2097152 | tf_op jit(solution)/shard_map/query_rest/pallas_call | solution.py:258
Async XLA Ops:
  0.7 2.2 %copy-start.1 = (bf16[128,16384]{1,0:T(8,128)(2,1)S(1)}, bf16[128,16384]{1,0:T(8,128)(2,1)}, u32[]{:S(2)}) copy-start(bf16[128,16384]{1,0:T(8,128)(2,1)} %weight_ref.3) | copy-start | bytes 12582916
  2.9 0.7 copy-start.2
  4.9 9.5 %collective-permute-start = (bf16[3,16,64,128]{3,2,1,0:T(8,128)(2,1)S(1)}, bf16[3,16,64,128]{3,2,1,0:T(8,128)(2,1)S(1)}, u32[]{:S(2)}, u32[]{:S(2)}) collective-permute-start(bf16[3,16,64,128]{3,2,1,0:T(8,128)(2,1)S(1)} %get-tuple-element.20), channel_id=1, source_target_pairs={{0,1},{1,0},{2,3},{3,2},{4,5},{5,4},{6,7},{7,6},{8,9},{9,8},{10,11... | collective-permute-start | bytes 2359304 | tf_op jit(solution)/shard_map/ppermute | solution.py:305
  5.6 2.3 %collective-permute-start.1 = (bf16[16,64,128]{2,1,0:T(8,128)(2,1)S(1)}, bf16[16,64,128]{2,1,0:T(8,128)(2,1)S(1)}, u32[]{:S(2)}, u32[]{:S(2)}) collective-permute-start(bf16[16,64,128]{2,1,0:T(8,128)(2,1)S(1)} %get-tuple-element.22), channel_id=1, source_target_pairs={{0,1},{1,0},{2,3},{3,2},{4,5},{5,4},{6,7},{7,6},{8,9},{9,8},{10,11... | collective-permute-start | bytes 786440 | tf_op jit(solution)/shard_map/ppermute | solution.py:305
  8.0 6.5 %collective-permute-start.2 = (bf16[8,64,128]{2,1,0:T(8,128)(2,1)S(1)}, bf16[8,64,128]{2,1,0:T(8,128)(2,1)S(1)}, u32[]{:S(2)}, u32[]{:S(2)}) collective-permute-start(bf16[8,64,128]{2,1,0:T(8,128)(2,1)S(1)} %get-tuple-element.23), channel_id=1, source_target_pairs={{0,2},{2,4},{4,6},{6,0},{1,3},{3,5},{5,7},{7,1},{8,10},{10,12},{12... | collective-permute-start | bytes 393224 | tf_op jit(solution)/shard_map/ppermute | solution.py:310
  9.4 5.0 %collective-permute-start.3 = (bf16[8,64,128]{2,1,0:T(8,128)(2,1)S(1)}, bf16[8,64,128]{2,1,0:T(8,128)(2,1)S(1)}, u32[]{:S(2)}, u32[]{:S(2)}) collective-permute-start(bf16[8,64,128]{2,1,0:T(8,128)(2,1)S(1)} %get-tuple-element.24), channel_id=1, source_target_pairs={{0,6},{2,0},{4,2},{6,4},{1,7},{3,1},{5,3},{7,5},{8,14},{10,8},{12,... | collective-permute-start | bytes 393224 | tf_op jit(solution)/shard_map/ppermute | solution.py:310
  14.6 45.2 %copy-start.3 = (bf16[64,128]{1,0:T(8,128)(2,1)S(1)}, bf16[64,128]{1,0:T(8,128)(2,1)}, u32[]{:S(2)}) copy-start(bf16[64,128]{1,0:T(8,128)(2,1)} %residual_ref.1) | copy-start | bytes 49156
  14.6 45.2 %copy-start.4 = (bf16[128]{0:T(256)(128)(2,1)S(1)}, bf16[128]{0:T(256)(128)(2,1)}, u32[]{:S(2)}) copy-start(bf16[128]{0:T(256)(128)(2,1)} %param.8) | copy-start | bytes 772
  14.7 8.2 %collective-permute-start.4 = (bf16[16,64,128]{2,1,0:T(8,128)(2,1)S(1)}, bf16[16,64,128]{2,1,0:T(8,128)(2,1)S(1)}, u32[]{:S(2)}, u32[]{:S(2)}) collective-permute-start(bf16[16,64,128]{2,1,0:T(8,128)(2,1)S(1)} %get-tuple-element.26), channel_id=1, source_target_pairs={{0,2},{2,4},{4,6},{6,0},{1,3},{3,5},{5,7},{7,1},{8,10},{10,12},{12... | collective-permute-start | bytes 786440 | tf_op jit(solution)/shard_map/ppermute | solution.py:310
  15.5 7.3 %collective-permute-start.5 = (bf16[16,64,128]{2,1,0:T(8,128)(2,1)S(1)}, bf16[16,64,128]{2,1,0:T(8,128)(2,1)S(1)}, u32[]{:S(2)}, u32[]{:S(2)}) collective-permute-start(bf16[16,64,128]{2,1,0:T(8,128)(2,1)S(1)} %get-tuple-element.27), channel_id=1, source_target_pairs={{0,6},{2,0},{4,2},{6,4},{1,7},{3,1},{5,3},{7,5},{8,14},{10,8},{12,... | collective-permute-start | bytes 786440 | tf_op jit(solution)/shard_map/ppermute | solution.py:310
  59.9 47.2 %copy-start = (bf16[16384,128]{1,0:T(8,128)(2,1)S(1)}, bf16[16384,128]{1,0:T(8,128)(2,1)}, u32[]{:S(2)}) copy-start(bf16[16384,128]{1,0:T(8,128)(2,1)} %weight_ref.5) | copy-start | bytes 12582916
  104.5 4.9 %collective-permute-start.6 = (bf16[4,1032,128]{2,1,0:T(8,128)(2,1)S(1)}, bf16[4,1032,128]{2,1,0:T(8,128)(2,1)S(1)}, u32[]{:S(2)}, u32[]{:S(2)}) collective-permute-start(bf16[4,1032,128]{2,1,0:T(8,128)(2,1)S(1)} %all_to_all.17.found_ref), channel_id=1, source_target_pairs={{0,1},{1,0},{2,3},{3,2},{4,5},{5,4},{6,7},{7,6},{8,9},{9,8},{10,11... | collective-permute-start | bytes 3170312 | tf_op jit(solution)/shard_map/ppermute | solution.py:305

commit v3 on v2

--- a/solution.py
+++ b/solution.py
@@ -11,6 +11,7 @@
 EPS = 1e-05
 TINY = 1e-06
 TOP = 448.0
+OPENING = 10000000000
 BF16, F32 = jnp.bfloat16, jnp.float32
 STAT_ROWS = 8
 NEAR = (1, -1, 0)
@@ -27,7 +28,23 @@
     return pl.CostEstimate(flops=flops, bytes_accessed=moved, transcendentals=0)
 
 
-def terms_kernel(dims, place_ref, heads_ref, weight_ref, far_sent_ref, far_mine_ref, near_sent_ref, near_mine_ref):
+def opening_kernel(place_ref, out_ref):
+    out_ref[...] = jnp.zeros_like(out_ref) + place_ref[0].astype(F32)
+
+
+def opening(place):
+    return pl.pallas_call(
+        opening_kernel,
+        out_shape=jax.ShapeDtypeStruct((8, 128), F32),
+        in_specs=[SMEM],
+        out_specs=VMEM,
+        compiler_params=params(16),
+        cost_estimate=cost(OPENING, OPENING),
+        name="opening",
+    )(place)
+
+
+def terms_kernel(dims, place_ref, heads_ref, weight_ref, after_ref, far_sent_ref, far_mine_ref, near_sent_ref, near_mine_ref):
     tp, tq, tr, width = dims
     core, here = place_ref[0], place_ref[1]
     span = tr * width
@@ -48,7 +65,7 @@
                 near_sent_ref[k - 1, t] = sent
 
 
-def all_terms(place, heads, weight, dims):
+def all_terms(place, heads, weight, after, dims):
     tp, _, _, width = dims
     tokens, _ = heads.shape
     far, near = (tp, tokens, width), (len(NEAR), tp, tokens, width)
@@ -60,12 +77,12 @@
             jax.ShapeDtypeStruct(near, BF16),
             jax.ShapeDtypeStruct(near, F32),
         ),
-        in_specs=[SMEM, VMEM, VMEM],
+        in_specs=[SMEM, VMEM, VMEM, ANY],
         out_specs=(VMEM,) * 4,
         compiler_params=params(16),
         cost_estimate=cost(2 * tokens * weight.size, 2 * weight.size),
         name="all_terms",
-    )(place, heads, weight)
+    )(place, heads, weight, after)
 
 
 def far_kernel(mine_ref, other_ref, right_ref, left_ref):
@@ -319,7 +336,9 @@
     here = lax.axis_index("tq").astype(jnp.int32)
     place = jnp.stack([core, here])
 
-    far_sent, far_mine, near_sent, near_mine = all_terms(place, attn_heads, o_weight, dims)
+    far_sent, far_mine, near_sent, near_mine = all_terms(
+        place, attn_heads, o_weight, opening(place), dims
+    )
     far_right, far_left = far_block(far_mine, swapped(far_sent))
     near_came = swapped(near_sent)
     left_got, right_got = moved(far_right, 1), moved(far_left, -1)

time: 111 us -> 110 us (level)
  local copies, waits for them, and re-layouts: 2.92 us -> 1.65 us
    unnamed x10, local copies, waits for them, and re-layouts: 2.92 us -> 1.65 us
where the time goes in v3:
time: 110 us
  blocking collectives  81.3 us (74%)
  waiting for transfers between devices  12.6 us (11%)
  starting transfers between devices  9.4 us (9%)
  Pallas kernels  4.14 us (4%)
  local copies, waits for them, and re-layouts  1.65 us (2%)
    all_to_all x3, blocking collectives, exchanged(): return lax.all_to_all(blocks, axis, split_axis=0, concat_axis=0, tiled=True)  81.3 us
    ppermute x4, waiting for transfers between devices, moved(): lax.ppermute(array, 'tq', [(k, (k + step) % size) for k in range(size)])  8.69 us
    ppermute x4, starting transfers between devices, moved(): lax.ppermute(array, 'tq', [(k, (k + step) % size) for k in range(size)])  5.96 us
    ppermute x3, waiting for transfers between devices, swapped(): return lax.ppermute(array, 'tr', [(0, 1), (1, 0)])  3.9 us
    ppermute x3, starting transfers between devices, swapped(): return lax.ppermute(array, 'tr', [(0, 1), (1, 0)])  3.45 us
  transfers between devices with their start and end apart: 7, of which 4 were waited for; matrix products, arithmetic and copies ran while one was open for 0% of the time, Pallas kernels for 1%

profile of v3, /device:TPU:161, one launch (start us, length us, event | category | flops | bytes accessed | tf_op | source)
XLA Modules:
  0.0 109.9 jit_solution(12145669403486896003)
XLA Ops:
  0.6 0.1 pad_add_fusion.place_ref
  0.7 0.0 copy-start.1
  0.7 0.0 copy-start.2
  0.7 0.5 opening.1.after_ref
  1.3 1.6 %copy-done.1 = bf16[128,16384]{1,0:T(8,128)(2,1)S(1)} copy-done((bf16[128,16384]{1,0:T(8,128)(2,1)S(1)}, bf16[128,16384]{1,0:T(8,128)(2,1)}, u32[]{:S(2)}) %copy-start.1) | copy-done | bytes 4194328
  2.9 0.0 copy-done.2
  2.9 1.3 %all_terms.1 = (bf16[16,64,128]{2,1,0:T(8,128)(2,1)S(1)}, f32[16,64,128]{2,1,0:T(8,128)S(1)}, bf16[3,16,64,128]{3,2,1,0:T(8,128)(2,1)S(1)}, f32[3,16,64,128]{3,2,1,0:T(8,128)S(1)}) custom-call(s32[2]{0:T(128)S(1)} %pad_add_fusion.place_ref, bf16[64,128]{1,0:T(8,128)(2,1)S(1)} %copy-done.2, bf16[128,16384]{1,0:T(8,128)(2,1)S(1)} %copy-done.1, ...), custom_call_target="tpu_custom_call" | custom-call | flops 268435456 | bytes 4194304 | tf_op jit(solution)/shard_map/all_terms/pallas_call | solution.py:72
  4.2 0.7 collective-permute-start
  4.9 0.1 collective-permute-start.1
  5.1 2.1 %collective-permute-done.1.other_ref = bf16[16,64,128]{2,1,0:T(8,128)(2,1)S(1)} collective-permute-done((bf16[16,64,128]{2,1,0:T(8,128)(2,1)S(1)}, bf16[16,64,128]{2,1,0:T(8,128)(2,1)S(1)}, u32[]{:S(2)}, u32[]{:S(2)}) %collective-permute-start.1) | collective-permute-done | bytes 262176 | tf_op jit(solution)/shard_map/ppermute | solution.py:322
  7.2 0.1 far_block.1
  7.3 1.5 %collective-permute-start.2 = (bf16[8,64,128]{2,1,0:T(8,128)(2,1)S(1)}, bf16[8,64,128]{2,1,0:T(8,128)(2,1)S(1)}, u32[]{:S(2)}, u32[]{:S(2)}) collective-permute-start(bf16[8,64,128]{2,1,0:T(8,128)(2,1)S(1)} %get-tuple-element.23), channel_id=1, source_target_pairs={{0,2},{2,4},{4,6},{6,0},{1,3},{3,5},{5,7},{7,1},{8,10},{10,12},{12... | collective-permute-start | bytes 393224 | tf_op jit(solution)/shard_map/ppermute | solution.py:327
  8.7 1.7 %collective-permute-start.3 = (bf16[8,64,128]{2,1,0:T(8,128)(2,1)S(1)}, bf16[8,64,128]{2,1,0:T(8,128)(2,1)S(1)}, u32[]{:S(2)}, u32[]{:S(2)}) collective-permute-start(bf16[8,64,128]{2,1,0:T(8,128)(2,1)S(1)} %get-tuple-element.24), channel_id=1, source_target_pairs={{0,6},{2,0},{4,2},{6,4},{1,7},{3,1},{5,3},{7,5},{8,14},{10,8},{12,... | collective-permute-start | bytes 393224 | tf_op jit(solution)/shard_map/ppermute | solution.py:327
  10.4 3.3 %collective-permute-done.2.left_got_ref = bf16[8,64,128]{2,1,0:T(8,128)(2,1)S(1)} collective-permute-done((bf16[8,64,128]{2,1,0:T(8,128)(2,1)S(1)}, bf16[8,64,128]{2,1,0:T(8,128)(2,1)S(1)}, u32[]{:S(2)}, u32[]{:S(2)}) %collective-permute-start.2) | collective-permute-done | bytes 131104 | tf_op jit(solution)/shard_map/ppermute | solution.py:327
  13.7 0.0 collective-permute-done.3.right_got_ref
  13.7 0.0 collective-permute-done.other_ref
  13.7 0.2 near_blocks.1
  13.9 0.0 copy-start.3
  13.9 0.0 copy-start.4
  13.9 0.8 collective-permute-start.4
  14.8 2.0 %collective-permute-start.5 = (bf16[16,64,128]{2,1,0:T(8,128)(2,1)S(1)}, bf16[16,64,128]{2,1,0:T(8,128)(2,1)S(1)}, u32[]{:S(2)}, u32[]{:S(2)}) collective-permute-start(bf16[16,64,128]{2,1,0:T(8,128)(2,1)S(1)} %get-tuple-element.27), channel_id=1, source_target_pairs={{0,6},{2,0},{4,2},{6,4},{1,7},{3,1},{5,3},{7,5},{8,14},{10,8},{12,... | collective-permute-start | bytes 786440 | tf_op jit(solution)/shard_map/ppermute | solution.py:327
  16.8 5.4 %collective-permute-done.4.left_ref = bf16[16,64,128]{2,1,0:T(8,128)(2,1)S(1)} collective-permute-done((bf16[16,64,128]{2,1,0:T(8,128)(2,1)S(1)}, bf16[16,64,128]{2,1,0:T(8,128)(2,1)S(1)}, u32[]{:S(2)}, u32[]{:S(2)}) %collective-permute-start.4) | collective-permute-done | bytes 262176 | tf_op jit(solution)/shard_map/ppermute | solution.py:327
  22.1 0.0 collective-permute-done.5.right_ref
  22.1 0.1 summed.1
  22.2 36.9 %all_to_all.15.parts_ref = bf16[16,64,128]{2,1,0:T(8,128)(2,1)S(1)} all-to-all(bf16[16,64,128]{2,1,0:T(8,128)(2,1)S(1)} %summed.1), channel_id=1, replica_groups=mesh['groups'=2,'tp'=16,'tq'=4,'tr'=2] {'tp'}, dimensions={0} | all-to-all | bytes 524288 | tf_op jit(solution)/shard_map/all_to_all | solution.py:318
  59.1 0.0 copy-done.3
  59.1 0.0 copy-done.4
  59.1 0.0 copy-start
  59.1 0.2 normed.1
  59.3 26.5 %all_to_all.16.line_ref = bf16[16,72,128]{2,1,0:T(8,128)(2,1)S(1)} all-to-all(bf16[16,72,128]{2,1,0:T(8,128)(2,1)S(1)} %get-tuple-element.28), channel_id=1, replica_groups=mesh['groups'=2,'tp'=16,'tq'=4,'tr'=2] {'tp'}, dimensions={0} | all-to-all | bytes 589824 | tf_op jit(solution)/shard_map/all_to_all | solution.py:318
  85.8 0.1 restacked.1
  85.9 17.9 %all_to_all.17.found_ref = bf16[4,1032,128]{2,1,0:T(8,128)(2,1)S(1)} all-to-all(bf16[4,1032,128]{2,1,0:T(8,128)(2,1)S(1)} %restacked.1), channel_id=1, replica_groups=mesh['groups'=2,'tp'=16,'tq'=4,'tr'=2] {'tq'}, dimensions={0} | all-to-all | bytes 2113536 | tf_op jit(solution)/shard_map/all_to_all | solution.py:318
  103.8 2.6 %collective-permute-start.6 = (bf16[4,1032,128]{2,1,0:T(8,128)(2,1)S(1)}, bf16[4,1032,128]{2,1,0:T(8,128)(2,1)S(1)}, u32[]{:S(2)}, u32[]{:S(2)}) collective-permute-start(bf16[4,1032,128]{2,1,0:T(8,128)(2,1)S(1)} %all_to_all.17.found_ref), channel_id=1, source_target_pairs={{0,1},{1,0},{2,3},{3,2},{4,5},{5,4},{6,7},{7,6},{8,9},{9,8},{10,11... | collective-permute-start | bytes 3170312 | tf_op jit(solution)/shard_map/ppermute | solution.py:322
  106.4 0.0 copy-done
  106.4 0.5 query_half.1
  106.9 1.8 %collective-permute-done.6.other_ref = bf16[4,1032,128]{2,1,0:T(8,128)(2,1)S(1)} collective-permute-done((bf16[4,1032,128]{2,1,0:T(8,128)(2,1)S(1)}, bf16[4,1032,128]{2,1,0:T(8,128)(2,1)S(1)}, u32[]{:S(2)}, u32[]{:S(2)}) %collective-permute-start.6) | collective-permute-done | bytes 1056800 | tf_op jit(solution)/shard_map/ppermute | solution.py:322
  108.7 1.2 %query_rest.1 = (bf16[64,128]{1,0:T(8,128)(2,1)}, f32[1,64]{1,0:T(1,128)}, bf16[64,128]{1,0:T(8,128)(2,1)}) custom-call(s32[1]{0:T(128)} %bitcast.core_ref, f32[64,128]{1,0:T(8,128)S(1)} %get-tuple-element.29.part_ref, f32[2,128]{1,0:T(2,128)S(1)} %get-tuple-element.30.stat_ref, bf16[4,1032,128]{2,1,0:T(8,128)(2,1)S(1)} %collective-permute-done.6.other_ref, ...), custom_call_target="tpu_custom_call" | custom-call | flops 134217728 | bytes 2097152 | tf_op jit(solution)/shard_map/query_rest/pallas_call | solution.py:275
Async XLA Ops:
  0.7 2.2 %copy-start.1 = (bf16[128,16384]{1,0:T(8,128)(2,1)S(1)}, bf16[128,16384]{1,0:T(8,128)(2,1)}, u32[]{:S(2)}) copy-start(bf16[128,16384]{1,0:T(8,128)(2,1)} %weight_ref.3) | copy-start | bytes 12582916
  0.7 2.2 %copy-start.2 = (bf16[64,128]{1,0:T(8,128)(2,1)S(1)}, bf16[64,128]{1,0:T(8,128)(2,1)}, u32[]{:S(2)}) copy-start(bf16[64,128]{1,0:T(8,128)(2,1)} %heads_ref.1) | copy-start | bytes 49156
  4.2 9.5 %collective-permute-start = (bf16[3,16,64,128]{3,2,1,0:T(8,128)(2,1)S(1)}, bf16[3,16,64,128]{3,2,1,0:T(8,128)(2,1)S(1)}, u32[]{:S(2)}, u32[]{:S(2)}) collective-permute-start(bf16[3,16,64,128]{3,2,1,0:T(8,128)(2,1)S(1)} %get-tuple-element.20), channel_id=1, source_target_pairs={{0,1},{1,0},{2,3},{3,2},{4,5},{5,4},{6,7},{7,6},{8,9},{9,8},{10,11... | collective-permute-start | bytes 2359304 | tf_op jit(solution)/shard_map/ppermute | solution.py:322
  4.9 2.3 %collective-permute-start.1 = (bf16[16,64,128]{2,1,0:T(8,128)(2,1)S(1)}, bf16[16,64,128]{2,1,0:T(8,128)(2,1)S(1)}, u32[]{:S(2)}, u32[]{:S(2)}) collective-permute-start(bf16[16,64,128]{2,1,0:T(8,128)(2,1)S(1)} %get-tuple-element.22), channel_id=1, source_target_pairs={{0,1},{1,0},{2,3},{3,2},{4,5},{5,4},{6,7},{7,6},{8,9},{9,8},{10,11... | collective-permute-start | bytes 786440 | tf_op jit(solution)/shard_map/ppermute | solution.py:322
  7.3 6.5 %collective-permute-start.2 = (bf16[8,64,128]{2,1,0:T(8,128)(2,1)S(1)}, bf16[8,64,128]{2,1,0:T(8,128)(2,1)S(1)}, u32[]{:S(2)}, u32[]{:S(2)}) collective-permute-start(bf16[8,64,128]{2,1,0:T(8,128)(2,1)S(1)} %get-tuple-element.23), channel_id=1, source_target_pairs={{0,2},{2,4},{4,6},{6,0},{1,3},{3,5},{5,7},{7,1},{8,10},{10,12},{12... | collective-permute-start | bytes 393224 | tf_op jit(solution)/shard_map/ppermute | solution.py:327
  8.7 5.0 %collective-permute-start.3 = (bf16[8,64,128]{2,1,0:T(8,128)(2,1)S(1)}, bf16[8,64,128]{2,1,0:T(8,128)(2,1)S(1)}, u32[]{:S(2)}, u32[]{:S(2)}) collective-permute-start(bf16[8,64,128]{2,1,0:T(8,128)(2,1)S(1)} %get-tuple-element.24), channel_id=1, source_target_pairs={{0,6},{2,0},{4,2},{6,4},{1,7},{3,1},{5,3},{7,5},{8,14},{10,8},{12,... | collective-permute-start | bytes 393224 | tf_op jit(solution)/shard_map/ppermute | solution.py:327
  13.9 45.2 %copy-start.3 = (bf16[64,128]{1,0:T(8,128)(2,1)S(1)}, bf16[64,128]{1,0:T(8,128)(2,1)}, u32[]{:S(2)}) copy-start(bf16[64,128]{1,0:T(8,128)(2,1)} %residual_ref.1) | copy-start | bytes 49156
  13.9 45.2 %copy-start.4 = (bf16[128]{0:T(256)(128)(2,1)S(1)}, bf16[128]{0:T(256)(128)(2,1)}, u32[]{:S(2)}) copy-start(bf16[128]{0:T(256)(128)(2,1)} %param.8) | copy-start | bytes 772
  13.9 8.2 %collective-permute-start.4 = (bf16[16,64,128]{2,1,0:T(8,128)(2,1)S(1)}, bf16[16,64,128]{2,1,0:T(8,128)(2,1)S(1)}, u32[]{:S(2)}, u32[]{:S(2)}) collective-permute-start(bf16[16,64,128]{2,1,0:T(8,128)(2,1)S(1)} %get-tuple-element.26), channel_id=1, source_target_pairs={{0,2},{2,4},{4,6},{6,0},{1,3},{3,5},{5,7},{7,1},{8,10},{10,12},{12... | collective-permute-start | bytes 786440 | tf_op jit(solution)/shard_map/ppermute | solution.py:327
  14.8 7.3 %collective-permute-start.5 = (bf16[16,64,128]{2,1,0:T(8,128)(2,1)S(1)}, bf16[16,64,128]{2,1,0:T(8,128)(2,1)S(1)}, u32[]{:S(2)}, u32[]{:S(2)}) collective-permute-start(bf16[16,64,128]{2,1,0:T(8,128)(2,1)S(1)} %get-tuple-element.27), channel_id=1, source_target_pairs={{0,6},{2,0},{4,2},{6,4},{1,7},{3,1},{5,3},{7,5},{8,14},{10,8},{12,... | collective-permute-start | bytes 786440 | tf_op jit(solution)/shard_map/ppermute | solution.py:327
  59.1 47.3 %copy-start = (bf16[16384,128]{1,0:T(8,128)(2,1)S(1)}, bf16[16384,128]{1,0:T(8,128)(2,1)}, u32[]{:S(2)}) copy-start(bf16[16384,128]{1,0:T(8,128)(2,1)} %weight_ref.5) | copy-start | bytes 12582916
  103.8 4.9 %collective-permute-start.6 = (bf16[4,1032,128]{2,1,0:T(8,128)(2,1)S(1)}, bf16[4,1032,128]{2,1,0:T(8,128)(2,1)S(1)}, u32[]{:S(2)}, u32[]{:S(2)}) collective-permute-start(bf16[4,1032,128]{2,1,0:T(8,128)(2,1)S(1)} %all_to_all.17.found_ref), channel_id=1, source_target_pairs={{0,1},{1,0},{2,3},{3,2},{4,5},{5,4},{6,7},{7,6},{8,9},{9,8},{10,11... | collective-permute-start | bytes 3170312 | tf_op jit(solution)/shard_map/ppermute | solution.py:322

commit v4 on v3

--- a/solution.py
+++ b/solution.py
@@ -44,44 +44,33 @@
     )(place)
 
 
-def terms_kernel(dims, place_ref, heads_ref, weight_ref, after_ref, far_sent_ref, far_mine_ref, near_sent_ref, near_mine_ref):
+def terms_kernel(dims, steps, place_ref, heads_ref, weight_ref, after_ref, sent_ref, mine_ref):
     tp, tq, tr, width = dims
     core, here = place_ref[0], place_ref[1]
     span = tr * width
     heads = heads_ref[...]
     for t in range(tp):
-        for k, step in enumerate((tq // 2,) + NEAR):
+        for k, step in enumerate(steps):
             q = lax.rem(here + (step + tq), tq)
             columns = pl.ds(pl.multiple_of((t * tq + q) * span, span), span)
             terms = jnp.dot(heads, weight_ref[:, columns], preferred_element_type=F32)
             low, high = terms[:, 0:width], terms[:, width:span]
-            mine = jnp.where(core == 0, low, high)
-            sent = jnp.where(core == 0, high, low).astype(BF16)
-            if k == 0:
-                far_mine_ref[t] = mine
-                far_sent_ref[t] = sent
-            else:
-                near_mine_ref[k - 1, t] = mine
-                near_sent_ref[k - 1, t] = sent
-
-
-def all_terms(place, heads, weight, after, dims):
+            mine_ref[k, t] = jnp.where(core == 0, low, high)
+            sent_ref[k, t] = jnp.where(core == 0, high, low).astype(BF16)
+
+
+def some_terms(place, heads, weight, after, dims, steps):
     tp, _, _, width = dims
     tokens, _ = heads.shape
-    far, near = (tp, tokens, width), (len(NEAR), tp, tokens, width)
-    return pl.pallas_call(
-        functools.partial(terms_kernel, dims),
-        out_shape=(
-            jax.ShapeDtypeStruct(far, BF16),
-            jax.ShapeDtypeStruct(far, F32),
-            jax.ShapeDtypeStruct(near, BF16),
-            jax.ShapeDtypeStruct(near, F32),
-        ),
+    shape = (len(steps), tp, tokens, width)
+    return pl.pallas_call(
+        functools.partial(terms_kernel, dims, steps),
+        out_shape=(jax.ShapeDtypeStruct(shape, BF16), jax.ShapeDtypeStruct(shape, F32)),
         in_specs=[SMEM, VMEM, VMEM, ANY],
-        out_specs=(VMEM,) * 4,
+        out_specs=(VMEM,) * 2,
         compiler_params=params(16),
         cost_estimate=cost(2 * tokens * weight.size, 2 * weight.size),
-        name="all_terms",
+        name="some_terms",
     )(place, heads, weight, after)
 
 
@@ -336,9 +325,10 @@
     here = lax.axis_index("tq").astype(jnp.int32)
     place = jnp.stack([core, here])
 
-    far_sent, far_mine, near_sent, near_mine = all_terms(
-        place, attn_heads, o_weight, opening(place), dims
-    )
+    first = opening(place)
+    far_sent, far_mine = some_terms(place, attn_heads, o_weight, first, dims, (tq // 2,))
+    far_sent, far_mine = far_sent[0], far_mine[0]
+    near_sent, near_mine = some_terms(place, attn_heads, o_weight, far_mine, dims, NEAR)
     far_right, far_left = far_block(far_mine, swapped(far_sent))
     near_came = swapped(near_sent)
     left_got, right_got = moved(far_right, 1), moved(far_left, -1)

time: 110 us -> 111 us (level)
  no operation moved by 1% of the time
where the time goes in v4:
time: 111 us
  blocking collectives  81.3 us (73%)
  waiting for transfers between devices  12.6 us (11%)
  starting transfers between devices  9.4 us (8%)
  Pallas kernels  4.85 us (4%)
  local copies, waits for them, and re-layouts  1.65 us (1%)
    all_to_all x3, blocking collectives, exchanged(): return lax.all_to_all(blocks, axis, split_axis=0, concat_axis=0, tiled=True)  81.3 us
    ppermute x4, waiting for transfers between devices, moved(): lax.ppermute(array, 'tq', [(k, (k + step) % size) for k in range(size)])  8.71 us
    ppermute x4, starting transfers between devices, moved(): lax.ppermute(array, 'tq', [(k, (k + step) % size) for k in range(size)])  5.96 us
    ppermute x3, waiting for transfers between devices, swapped(): return lax.ppermute(array, 'tr', [(0, 1), (1, 0)])  3.9 us
    ppermute x3, starting transfers between devices, swapped(): return lax.ppermute(array, 'tr', [(0, 1), (1, 0)])  3.45 us
  transfers between devices with their start and end apart: 7, of which 4 were waited for; matrix products, arithmetic and copies ran while one was open for 0% of the time, Pallas kernels for 1%

profile of v4, /device:TPU:161, one launch (start us, length us, event | category | flops | bytes accessed | tf_op | source)
XLA Modules:
  0.0 110.6 jit_solution(3069263886318790515)
XLA Ops:
  0.6 0.1 pad_add_fusion.place_ref
  0.7 0.0 copy-start
  0.7 0.0 copy-start.2
  0.7 0.5 opening.1.after_ref
  1.3 1.6 %copy-done = bf16[128,16384]{1,0:T(8,128)(2,1)S(1)} copy-done((bf16[128,16384]{1,0:T(8,128)(2,1)S(1)}, bf16[128,16384]{1,0:T(8,128)(2,1)}, u32[]{:S(2)}) %copy-start) | copy-done | bytes 4194328
  2.9 0.0 copy-done.2
  2.9 0.9 some_terms.2
  3.8 1.1 %some_terms.3 = (bf16[3,16,64,128]{3,2,1,0:T(8,128)(2,1)S(1)}, f32[3,16,64,128]{3,2,1,0:T(8,128)S(1)}) custom-call(s32[2]{0:T(128)S(1)} %pad_add_fusion.place_ref, bf16[64,128]{1,0:T(8,128)(2,1)S(1)} %copy-done.2, bf16[128,16384]{1,0:T(8,128)(2,1)S(1)} %copy-done, f32[16,64,128]{2,1,0:T(8,128)S(1)} %bitcast.6), custom_call_target="tpu_custom_call" | custom-call | flops 268435456 | bytes 4194304 | tf_op jit(solution)/shard_map/some_terms/pallas_call | solution.py:66
  4.9 0.7 collective-permute-start
  5.6 0.1 collective-permute-start.1
  5.8 2.1 %collective-permute-done.1.other_ref = bf16[16,64,128]{2,1,0:T(8,128)(2,1)S(1)} collective-permute-done((bf16[16,64,128]{2,1,0:T(8,128)(2,1)S(1)}, bf16[16,64,128]{2,1,0:T(8,128)(2,1)S(1)}, u32[]{:S(2)}, u32[]{:S(2)}) %collective-permute-start.1) | collective-permute-done | bytes 262176 | tf_op jit(solution)/shard_map/ppermute | solution.py:311
  8.0 1.5 %collective-permute-start.2 = (bf16[8,64,128]{2,1,0:T(8,128)(2,1)S(1)}, bf16[8,64,128]{2,1,0:T(8,128)(2,1)S(1)}, u32[]{:S(2)}, u32[]{:S(2)}) collective-permute-start(bf16[8,64,128]{2,1,0:T(8,128)(2,1)S(1)} %get-tuple-element.23), channel_id=1, source_target_pairs={{0,2},{2,4},{4,6},{6,0},{1,3},{3,5},{5,7},{7,1},{8,10},{10,12},{12... | collective-permute-start | bytes 393224 | tf_op jit(solution)/shard_map/ppermute | solution.py:316
  9.4 1.7 %collective-permute-start.3 = (bf16[8,64,128]{2,1,0:T(8,128)(2,1)S(1)}, bf16[8,64,128]{2,1,0:T(8,128)(2,1)S(1)}, u32[]{:S(2)}, u32[]{:S(2)}) collective-permute-start(bf16[8,64,128]{2,1,0:T(8,128)(2,1)S(1)} %get-tuple-element.24), channel_id=1, source_target_pairs={{0,6},{2,0},{4,2},{6,4},{1,7},{3,1},{5,3},{7,5},{8,14},{10,8},{12,... | collective-permute-start | bytes 393224 | tf_op jit(solution)/shard_map/ppermute | solution.py:316
  11.1 3.3 %collective-permute-done.2.left_got_ref = bf16[8,64,128]{2,1,0:T(8,128)(2,1)S(1)} collective-permute-done((bf16[8,64,128]{2,1,0:T(8,128)(2,1)S(1)}, bf16[8,64,128]{2,1,0:T(8,128)(2,1)S(1)}, u32[]{:S(2)}, u32[]{:S(2)}) %collective-permute-start.2) | collective-permute-done | bytes 131104 | tf_op jit(solution)/shard_map/ppermute | solution.py:316
  14.4 0.0 collective-permute-done.3.right_got_ref
  14.4 0.0 collective-permute-done.other_ref
  14.4 0.2 near_blocks.1
  14.6 0.0 copy-start.3
  14.7 0.0 copy-start.4
  14.7 0.9 collective-permute-start.4
  15.5 2.0 %collective-permute-start.5 = (bf16[16,64,128]{2,1,0:T(8,128)(2,1)S(1)}, bf16[16,64,128]{2,1,0:T(8,128)(2,1)S(1)}, u32[]{:S(2)}, u32[]{:S(2)}) collective-permute-start(bf16[16,64,128]{2,1,0:T(8,128)(2,1)S(1)} %get-tuple-element.27), channel_id=1, source_target_pairs={{0,6},{2,0},{4,2},{6,4},{1,7},{3,1},{5,3},{7,5},{8,14},{10,8},{12,... | collective-permute-start | bytes 786440 | tf_op jit(solution)/shard_map/ppermute | solution.py:316
  17.5 5.4 %collective-permute-done.4.left_ref = bf16[16,64,128]{2,1,0:T(8,128)(2,1)S(1)} collective-permute-done((bf16[16,64,128]{2,1,0:T(8,128)(2,1)S(1)}, bf16[16,64,128]{2,1,0:T(8,128)(2,1)S(1)}, u32[]{:S(2)}, u32[]{:S(2)}) %collective-permute-start.4) | collective-permute-done | bytes 262176 | tf_op jit(solution)/shard_map/ppermute | solution.py:316
  22.9 0.0 collective-permute-done.5.right_ref
  22.9 0.1 summed.1
  22.9 36.9 %all_to_all.15.parts_ref = bf16[16,64,128]{2,1,0:T(8,128)(2,1)S(1)} all-to-all(bf16[16,64,128]{2,1,0:T(8,128)(2,1)S(1)} %summed.1), channel_id=1, replica_groups=mesh['groups'=2,'tp'=16,'tq'=4,'tr'=2] {'tp'}, dimensions={0} | all-to-all | bytes 524288 | tf_op jit(solution)/shard_map/all_to_all | solution.py:307
  59.9 0.0 copy-done.3
  59.9 0.0 copy-done.4
  59.9 0.0 copy-start.1
  59.9 0.2 normed.1
  60.0 26.4 %all_to_all.16.line_ref = bf16[16,72,128]{2,1,0:T(8,128)(2,1)S(1)} all-to-all(bf16[16,72,128]{2,1,0:T(8,128)(2,1)S(1)} %get-tuple-element.28), channel_id=1, replica_groups=mesh['groups'=2,'tp'=16,'tq'=4,'tr'=2] {'tp'}, dimensions={0} | all-to-all | bytes 589824 | tf_op jit(solution)/shard_map/all_to_all | solution.py:307
  86.4 0.1 restacked.1
  86.5 18.0 %all_to_all.17.found_ref = bf16[4,1032,128]{2,1,0:T(8,128)(2,1)S(1)} all-to-all(bf16[4,1032,128]{2,1,0:T(8,128)(2,1)S(1)} %restacked.1), channel_id=1, replica_groups=mesh['groups'=2,'tp'=16,'tq'=4,'tr'=2] {'tq'}, dimensions={0} | all-to-all | bytes 2113536 | tf_op jit(solution)/shard_map/all_to_all | solution.py:307
  104.5 2.6 %collective-permute-start.6 = (bf16[4,1032,128]{2,1,0:T(8,128)(2,1)S(1)}, bf16[4,1032,128]{2,1,0:T(8,128)(2,1)S(1)}, u32[]{:S(2)}, u32[]{:S(2)}) collective-permute-start(bf16[4,1032,128]{2,1,0:T(8,128)(2,1)S(1)} %all_to_all.17.found_ref), channel_id=1, source_target_pairs={{0,1},{1,0},{2,3},{3,2},{4,5},{5,4},{6,7},{7,6},{8,9},{9,8},{10,11... | collective-permute-start | bytes 3170312 | tf_op jit(solution)/shard_map/ppermute | solution.py:311
  107.1 0.0 copy-done.1
  107.1 0.5 query_half.1
  107.7 1.8 %collective-permute-done.6.other_ref = bf16[4,1032,128]{2,1,0:T(8,128)(2,1)S(1)} collective-permute-done((bf16[4,1032,128]{2,1,0:T(8,128)(2,1)S(1)}, bf16[4,1032,128]{2,1,0:T(8,128)(2,1)S(1)}, u32[]{:S(2)}, u32[]{:S(2)}) %collective-permute-start.6) | collective-permute-done | bytes 1056800 | tf_op jit(solution)/shard_map/ppermute | solution.py:311
  109.4 1.2 %query_rest.1 = (bf16[64,128]{1,0:T(8,128)(2,1)}, f32[1,64]{1,0:T(1,128)}, bf16[64,128]{1,0:T(8,128)(2,1)}) custom-call(s32[1]{0:T(128)} %bitcast.core_ref, f32[64,128]{1,0:T(8,128)S(1)} %get-tuple-element.29.part_ref, f32[2,128]{1,0:T(2,128)S(1)} %get-tuple-element.30.stat_ref, bf16[4,1032,128]{2,1,0:T(8,128)(2,1)S(1)} %collective-permute-done.6.other_ref, ...), custom_call_target="tpu_custom_call" | custom-call | flops 134217728 | bytes 2097152 | tf_op jit(solution)/shard_map/query_rest/pallas_call | solution.py:264
  (1 shorter events, 0.0 us)
Async XLA Ops:
  0.7 2.2 %copy-start = (bf16[128,16384]{1,0:T(8,128)(2,1)S(1)}, bf16[128,16384]{1,0:T(8,128)(2,1)}, u32[]{:S(2)}) copy-start(bf16[128,16384]{1,0:T(8,128)(2,1)} %weight_ref.5) | copy-start | bytes 12582916
  0.7 2.2 %copy-start.2 = (bf16[64,128]{1,0:T(8,128)(2,1)S(1)}, bf16[64,128]{1,0:T(8,128)(2,1)}, u32[]{:S(2)}) copy-start(bf16[64,128]{1,0:T(8,128)(2,1)} %heads_ref.3) | copy-start | bytes 49156
  4.9 9.5 %collective-permute-start = (bf16[3,16,64,128]{3,2,1,0:T(8,128)(2,1)S(1)}, bf16[3,16,64,128]{3,2,1,0:T(8,128)(2,1)S(1)}, u32[]{:S(2)}, u32[]{:S(2)}) collective-permute-start(bf16[3,16,64,128]{3,2,1,0:T(8,128)(2,1)S(1)} %get-tuple-element.21), channel_id=1, source_target_pairs={{0,1},{1,0},{2,3},{3,2},{4,5},{5,4},{6,7},{7,6},{8,9},{9,8},{10,11... | collective-permute-start | bytes 2359304 | tf_op jit(solution)/shard_map/ppermute | solution.py:311
  5.6 2.3 %collective-permute-start.1 = (bf16[16,64,128]{2,1,0:T(8,128)(2,1)S(1)}, bf16[16,64,128]{2,1,0:T(8,128)(2,1)S(1)}, u32[]{:S(2)}, u32[]{:S(2)}) collective-permute-start(bf16[16,64,128]{2,1,0:T(8,128)(2,1)S(1)} %bitcast.9), channel_id=1, source_target_pairs={{0,1},{1,0},{2,3},{3,2},{4,5},{5,4},{6,7},{7,6},{8,9},{9,8},{10,11... | collective-permute-start | bytes 786440 | tf_op jit(solution)/shard_map/ppermute | solution.py:311
  8.0 6.5 %collective-permute-start.2 = (bf16[8,64,128]{2,1,0:T(8,128)(2,1)S(1)}, bf16[8,64,128]{2,1,0:T(8,128)(2,1)S(1)}, u32[]{:S(2)}, u32[]{:S(2)}) collective-permute-start(bf16[8,64,128]{2,1,0:T(8,128)(2,1)S(1)} %get-tuple-element.23), channel_id=1, source_target_pairs={{0,2},{2,4},{4,6},{6,0},{1,3},{3,5},{5,7},{7,1},{8,10},{10,12},{12... | collective-permute-start | bytes 393224 | tf_op jit(solution)/shard_map/ppermute | solution.py:316
  9.4 5.0 %collective-permute-start.3 = (bf16[8,64,128]{2,1,0:T(8,128)(2,1)S(1)}, bf16[8,64,128]{2,1,0:T(8,128)(2,1)S(1)}, u32[]{:S(2)}, u32[]{:S(2)}) collective-permute-start(bf16[8,64,128]{2,1,0:T(8,128)(2,1)S(1)} %get-tuple-element.24), channel_id=1, source_target_pairs={{0,6},{2,0},{4,2},{6,4},{1,7},{3,1},{5,3},{7,5},{8,14},{10,8},{12,... | collective-permute-start | bytes 393224 | tf_op jit(solution)/shard_map/ppermute | solution.py:316
  14.6 45.2 %copy-start.3 = (bf16[64,128]{1,0:T(8,128)(2,1)S(1)}, bf16[64,128]{1,0:T(8,128)(2,1)}, u32[]{:S(2)}) copy-start(bf16[64,128]{1,0:T(8,128)(2,1)} %residual_ref.1) | copy-start | bytes 49156
  14.7 45.2 %copy-start.4 = (bf16[128]{0:T(256)(128)(2,1)S(1)}, bf16[128]{0:T(256)(128)(2,1)}, u32[]{:S(2)}) copy-start(bf16[128]{0:T(256)(128)(2,1)} %param.8) | copy-start | bytes 772
  14.7 8.2 %collective-permute-start.4 = (bf16[16,64,128]{2,1,0:T(8,128)(2,1)S(1)}, bf16[16,64,128]{2,1,0:T(8,128)(2,1)S(1)}, u32[]{:S(2)}, u32[]{:S(2)}) collective-permute-start(bf16[16,64,128]{2,1,0:T(8,128)(2,1)S(1)} %get-tuple-element.26), channel_id=1, source_target_pairs={{0,2},{2,4},{4,6},{6,0},{1,3},{3,5},{5,7},{7,1},{8,10},{10,12},{12... | collective-permute-start | bytes 786440 | tf_op jit(solution)/shard_map/ppermute | solution.py:316
  15.5 7.3 %collective-permute-start.5 = (bf16[16,64,128]{2,1,0:T(8,128)(2,1)S(1)}, bf16[16,64,128]{2,1,0:T(8,128)(2,1)S(1)}, u32[]{:S(2)}, u32[]{:S(2)}) collective-permute-start(bf16[16,64,128]{2,1,0:T(8,128)(2,1)S(1)} %get-tuple-element.27), channel_id=1, source_target_pairs={{0,6},{2,0},{4,2},{6,4},{1,7},{3,1},{5,3},{7,5},{8,14},{10,8},{12,... | collective-permute-start | bytes 786440 | tf_op jit(solution)/shard_map/ppermute | solution.py:316
  59.9 47.2 %copy-start.1 = (bf16[16384,128]{1,0:T(8,128)(2,1)S(1)}, bf16[16384,128]{1,0:T(8,128)(2,1)}, u32[]{:S(2)}) copy-start(bf16[16384,128]{1,0:T(8,128)(2,1)} %weight_ref.7) | copy-start | bytes 12582916
  104.5 4.9 %collective-permute-start.6 = (bf16[4,1032,128]{2,1,0:T(8,128)(2,1)S(1)}, bf16[4,1032,128]{2,1,0:T(8,128)(2,1)S(1)}, u32[]{:S(2)}, u32[]{:S(2)}) collective-permute-start(bf16[4,1032,128]{2,1,0:T(8,128)(2,1)S(1)} %all_to_all.17.found_ref), channel_id=1, source_target_pairs={{0,1},{1,0},{2,3},{3,2},{4,5},{5,4},{6,7},{7,6},{8,9},{9,8},{10,11... | collective-permute-start | bytes 3170312 | tf_op jit(solution)/shard_map/ppermute | solution.py:311
